TPU v7x, 32 devices: a 4x4x1 block of a 4x4x8 slice. The times are simulated.
32 devices in a mesh: data: 1 (over z), cols: 4 (over y), model: 8 (over x, core).
Axes of the slice: x: 4, y: 4, z: 1, core: 2. Of those that a mesh axis runs over, the one named last changes fastest.
The devices are a block of a 4x4x8 slice.
Arguments:
- x_in: bfloat16 [64, 56, 56, 64], P('data', None, None, ('model', 'cols'))
- w_conv1: bfloat16 [3, 3, 64, 64], P(None, None, ('model', 'cols'))
- b_conv1: float32 [64], replicated
- w_conv2: bfloat16 [3, 3, 64, 64], replicated
- b_conv2: float32 [64], replicated
Outputs:
- output: float32 [64, 56, 56, 64], P('data', 'model', 'cols')
All inputs are finite; a program needn't handle non-finite values.
Results may differ from a plain program's by a relative error of at most 0.001.
Values are sent between devices in bfloat16 or wider.
A program may use at most 768 MiB of HBM per device.

v0:
```python
import jax
import jax.numpy as jnp
from jax import lax
from jax.sharding import PartitionSpec as P

CONV_DIMS = ("NHWC", "HWIO", "NHWC")
GROUP_AXES = ("model", "cols")


def halo_tiles(full, n_rows, n_cols):
    batch, height, width, channels = full.shape
    tile_h = height // n_rows
    tile_w = width // n_cols
    blocks = full.reshape(batch, n_rows, tile_h, width, channels)
    zero_row = jnp.zeros((batch, 1, width, channels), full.dtype)
    above = jnp.concatenate([zero_row, blocks[:, :-1, tile_h - 1]], axis=1)
    below = jnp.concatenate([blocks[:, 1:, 0], zero_row], axis=1)
    row_ext = jnp.concatenate([above[:, :, None], blocks, below[:, :, None]], axis=2)
    grid = row_ext.reshape(batch, n_rows, tile_h + 2, n_cols, tile_w, channels)
    zero_col = jnp.zeros((batch, n_rows, tile_h + 2, 1, channels), full.dtype)
    left = jnp.concatenate([zero_col, grid[:, :, :, :-1, tile_w - 1]], axis=3)
    right = jnp.concatenate([grid[:, :, :, 1:, 0], zero_col], axis=3)
    windows = jnp.concatenate([left[:, :, :, :, None], grid, right[:, :, :, :, None]], axis=4)
    windows = windows.transpose(1, 3, 0, 2, 4, 5)
    return windows.reshape(n_rows * n_cols, batch, tile_h + 2, tile_w + 2, channels)


def bias_relu(z_tile, bias, row_idx, col_idx, height, width):
    tile_h = z_tile.shape[1] - 2
    tile_w = z_tile.shape[2] - 2
    rows_at = row_idx * tile_h - 1 + jnp.arange(tile_h + 2)
    cols_at = col_idx * tile_w - 1 + jnp.arange(tile_w + 2)
    row_ok = (rows_at >= 0) & (rows_at < height)
    col_ok = (cols_at >= 0) & (cols_at < width)
    inside = row_ok[:, None, None] & col_ok[None, :, None]
    return jnp.where(inside, jnp.maximum(z_tile + bias, 0.0), 0.0).astype(jnp.bfloat16)


def solution(mesh):
    n_rows = mesh.shape["model"]
    n_cols = mesh.shape["cols"]

    def run_local(x_in, w_conv1, b_conv1, w_conv2, b_conv2):
        height = x_in.shape[1]
        width = x_in.shape[2]
        part_sum = lax.conv_general_dilated(x_in, w_conv1, (1, 1), "SAME", dimension_numbers=CONV_DIMS, preferred_element_type=jnp.float32)
        windows = halo_tiles(part_sum, n_rows, n_cols)
        z_tile = lax.psum_scatter(windows, GROUP_AXES, scatter_dimension=0, tiled=False)
        act_tile = bias_relu(z_tile, b_conv1, lax.axis_index("model"), lax.axis_index("cols"), height, width)
        out_tile = lax.conv_general_dilated(act_tile, w_conv2, (1, 1), "VALID", dimension_numbers=CONV_DIMS, preferred_element_type=jnp.float32)
        return out_tile + b_conv2

    return jax.shard_map(
        run_local,
        mesh=mesh,
        in_specs=(P("data", None, None, GROUP_AXES), P(None, None, GROUP_AXES, None), P(), P(), P()),
        out_specs=P("data", "model", "cols", None),
        check_vma=False,
    )
```

profile of v0, /device:TPU:97, one launch (start us, length us, event | category | flops | bytes accessed | tf_op | source)
XLA Modules:
  0.0 913.4 jit_solution(10238810462755141452)
XLA Ops:
  6.5 0.0 copy-start
  6.6 0.0 reduce-scatter.2.cloned.1.call-start
  6.6 1.4 copy-done
  8.0 37.7 %fusion.13 = f32[64,56,56,64]{3,0,2,1:T(8,128)} fusion(bf16[64,56,56,2]{0,3,2,1:T(2,128)(2,1)S(1)} %copy-done, bf16[3,3,2,64]{3,2,1,0:T(2,128)(2,1)} %param.6), kind=kOutput, calls=%fused_computation.22 | convolution fusion | flops 451477504 | bytes 52185344 | tf_op jit(solution)/shard_map/conv_general_dilated | solution.py:46
  45.7 19.6 %slice_bitcast_fusion.1 = (f32[64,7,56,64]{3,0,2,1:T(8,128)}, f32[64,7,56,64]{3,0,2,1:T(8,128)}) fusion(f32[64,8,7,56,64]{4,0,3,2,1:T(8,128)} %bitcast), kind=kLoop, calls=%fused_computation.2 | loop fusion | bytes 25690112 | tf_op jit(solution)/shard_map/squeeze | solution.py:16
  65.3 13.0 %concatenate.25 = f32[64,8,56,64]{3,0,2,1:T(8,128)} pad(f32[64,7,56,64]{3,0,2,1:T(8,128)} %get-tuple-element.7, f32[]{:T(128)} %constant.6.clone.1), padding=0_0x1_0x0_0x0_0 | pad | bytes 13762564 | tf_op jit(solution)/shard_map/concatenate | solution.py:16
  78.3 13.1 %concatenate.28 = f32[64,8,56,64]{3,0,2,1:T(8,128)} pad(f32[64,7,56,64]{3,0,2,1:T(8,128)} %get-tuple-element.8, f32[]{:T(128)} %constant.6.clone.1), padding=0_0x0_1x0_0x0_0 | pad | bytes 13762564 | tf_op jit(solution)/shard_map/concatenate | solution.py:17
  91.5 6.2 maximum_bitcast_fusion.1
  97.7 7.5 pad_bitcast_fusion
  105.2 97.0 %maximum_bitcast_fusion = f32[8,4,64,9,16,64]{5,2,4,1,3,0:T(8,128)} fusion(f32[64,8,9,4,1,64]{5,0,4,3,2,1:T(8,128)} %get-tuple-element.9, f32[64,8,1,4,14,64]{5,0,4,3,2,1:T(8,128)} %bitcast.40, f32[64,8,7,4,14,64]{5,0,4,3,2,1:T(8,128)} %bitcast.3, f32[64,8,1,4,14,64]{5,0,4,3,2,1:T(8,128)} %bitcast.38, f32[64,8,9,4,1,64]{5,0,4,3,2,1:T(8,128)} %get-tuple-element.10), kind=kLoop, calls=%fused_computation | loop fusion | flops 75497472 | bytes 150994944 | tf_op jit(solution)/shard_map/transpose | solution.py:24
  202.2 98.5 %copy.8 = f32[8,4,64,9,16,64]{5,2,4,3,1,0:T(8,128)} copy(f32[8,4,64,9,16,64]{5,2,4,1,3,0:T(8,128)} %maximum_bitcast_fusion) | data formatting | bytes 150994944 | tf_op jit(solution)/shard_map/transpose | solution.py:24
  300.7 0.0 copy-start.2
  300.7 0.0 copy-start.3
  300.7 0.0 copy-start.4
  300.7 0.1 reduce-scatter.2.cloned.1.call-update
  300.8 0.0 copy-start.1
  300.8 0.1 broadcast_and_fusion
  300.9 598.5 %reduce-scatter.2.cloned.1.call-done = f32[1,64,9,16,64]{4,1,3,2,0:T(8,128)} async-done(((f32[32,64,9,16,64]{4,1,3,2,0:T(8,128)}), f32[1,64,9,16,64]{4,1,3,2,0:T(8,128)}) %reduce-scatter.2.cloned.1.call-update) | async-done | bytes 2359312 | tf_op jit(solution)/shard_map/reduce_scatter | solution.py:48
  899.4 0.0 copy-done.2
  899.4 0.0 copy-done.3
  899.4 0.0 copy-done.4
  899.4 7.2 fusion.9
  906.5 0.0 copy-done.1
  (2 shorter events, 0.0 us)
Async XLA Ops:
  6.5 1.4 copy-start
  6.6 892.8 %reduce-scatter.2.cloned.1.call-start = ((), (), s32[]{:S(2)}) async-start(), calls=%async_computation.1 | async-start | bytes 155713536 | tf_op jit(solution)/shard_map/reduce_scatter | solution.py:48
  300.7 598.7 %copy-start.2 = (bf16[3,3,64,64]{3,2,1,0:T(8,128)(2,1)S(1)}, bf16[3,3,64,64]{3,2,1,0:T(8,128)(2,1)}, u32[]{:S(2)}) copy-start(bf16[3,3,64,64]{3,2,1,0:T(8,128)(2,1)} %param.8) | copy-start | bytes 221188
  300.7 598.7 %copy-start.3 = (f32[64]{0:T(128)S(1)}, f32[64]{0:T(128)}, u32[]{:S(2)}) copy-start(f32[64]{0:T(128)} %param.7) | copy-start | bytes 772
  300.7 598.7 %copy-start.4 = (f32[64]{0:T(128)S(1)}, f32[64]{0:T(128)}, u32[]{:S(2)}) copy-start(f32[64]{0:T(128)} %param.9) | copy-start | bytes 772
  300.8 605.7 %copy-start.1 = (bf16[64,56,56,2]{0,3,2,1:T(2,128)(2,1)S(1)}, bf16[64,56,56,2]{0,3,2,1:T(2,128)(2,1)}, u32[]{:S(2)}) copy-start(bf16[64,56,56,2]{0,3,2,1:T(2,128)(2,1)} %param.5) | copy-start | bytes 2408452
Sparse Core Ops, SparseCore 0:
  300.9 598.4 reduce-scatter.1
where the time goes:
time: 914 us; the launch traced here: 913 us
  waiting for transfers between devices  599 us (66%)
  local copies, waits for them, and re-layouts  153 us (17%)
  other arithmetic  103 us (11%)
  matrix products  44.9 us (5%)
  between operations  13.5 us (1%)
    reduce_scatter x1, waiting for transfers between devices, run_local(): lax.psum_scatter(windows, GROUP_AXES, scatter_dimension=0, tiled=False)  598 us
    transpose x1, local copies, waits for them, and re-layouts, halo_tiles(): windows = windows.transpose(1, 3, 0, 2, 4, 5)  98.5 us
    transpose x1, other arithmetic, halo_tiles(): windows = windows.transpose(1, 3, 0, 2, 4, 5)  97 us
    conv_general_dilated x1, matrix products, run_local(): lax.conv_general_dilated(x_in, w_conv1, (1, 1), 'SAME', dimension_numbers...  37.7 us
    squeeze x1, local copies, waits for them, and re-layouts, halo_tiles(): above = jnp.concatenate([zero_row, blocks[:, :-1, tile_h - 1]], axis=1)  19.6 us
  transfers between devices with their start and end apart: 1, of which 1 were waited for; matrix products, arithmetic and copies ran while one was open for 0% of the time, Pallas kernels for 0%

commit v1 on v0

v1 whole, which is shorter than its diff:
```python
import functools

import jax
import jax.numpy as jnp
from jax import lax
from jax.experimental import pallas as pl
from jax.experimental.pallas import tpu as pltpu
from jax.sharding import PartitionSpec as P

MESH = pl.DeviceIdType.MESH
BF16 = jnp.bfloat16
F32 = jnp.float32
FIRST_ROWS = 3
AHEAD = (1, 0)
COLUMN_FIRST = (2, 3)
CHIPS_ALONG = (1, 3, 2, 0)
CHIP_ORDER = tuple((other, dy) for other in (0, 1) for dy in (1, -1, 0, 2))


def turn(recv, i, put):
    sources, _, win_j, own_chans, lanes = recv.shape
    chans = sources * own_chans
    for j in range(win_j):
        top = recv[:, 2 * i, j].reshape(chans, lanes)
        under = recv[:, 2 * i + 1, j].reshape(chans, lanes)
        put(j, jnp.concatenate([top, under], axis=0).T.reshape(2, lanes // 2, 2 * chans))


def blocks(pairs, weights, count):
    acc = None
    for dw in range(4):
        parts = [view[dw // 2 : dw // 2 + count, dw % 2] for view in pairs]
        lhs = jnp.concatenate([p.reshape(count * p.shape[1], p.shape[2]) for p in parts], axis=1)
        term = jnp.dot(lhs, weights(dw), preferred_element_type=F32)
        acc = term if acc is None else acc + term
    return acc


def first(pairs, weights, bias, y_row, blank_a):
    count, _, images, lanes = y_row.shape
    c = lax.axis_index("cols")
    row = lax.rem(lax.broadcasted_iota(jnp.int32, (1, 2 * lanes), 1), lanes) // (lanes // 2)
    act = jnp.maximum(blocks(pairs, weights, count) + bias, 0.0)
    act = jnp.where(row != blank_a, act, 0.0).astype(BF16)
    for b in range(2):
        y_row[:, b] = act[:, b * lanes : (b + 1) * lanes].reshape(count, images, lanes)
    blank = jnp.zeros((images, lanes), BF16)

    @pl.when(c == 0)
    def _():
        y_row[0, 0] = blank

    @pl.when(c == lax.axis_size("cols") - 1)
    def _():
        y_row[count - 1, 1] = blank


def second(pairs, weights, bias, out_pair):
    _, count, _, images, chans = out_pair.shape
    res = blocks(pairs, weights, count) + bias
    for b in range(2):
        for a in range(2):
            at = (2 * b + a) * chans
            out_pair[a, :, b] = res[:, at : at + chans].reshape(count, images, chans)


def conv_kernel(
    n_rows,
    n_cols,
    x_hbm,
    w1_hbm,
    b1_hbm,
    w2_hbm,
    b2_hbm,
    out,
    ymat,
    wt2,
    bias2,
    recv,
    xmat,
    wt1,
    bias1,
    xs,
    packed,
    w1s,
    w1own,
    w1all,
    w2s,
    b1s,
    b2s,
    load_sem,
    par_sem,
    send_sem,
    recv_sem,
    wsend_sem,
    wrecv_sem,
    swap_send_sem,
    swap_recv_sem,
    wswap_send_sem,
    wswap_recv_sem,
):
    chip_h, pairs = xs.shape[1:3]
    images = xs.shape[-1]
    tile_h, tile_j = chip_h // 2, pairs // n_cols
    win_j = tile_j + 2
    sources = n_rows * n_cols
    r, c = lax.axis_index("model"), lax.axis_index("cols")
    par = lax.rem(r, 2)
    me = r * n_cols + c
    chans = recv.shape[0] * 2

    near = tile_h - FIRST_ROWS
    groups = (((near, chip_h - near),), *(((k, k + 2), (chip_h - k - 2, chip_h - k)) for k in range(near - 2, -1, -2)))
    loads = []
    for g, spans in enumerate(groups):
        loads.append(
            [
                pltpu.make_async_copy(x_hbm.at[:, lo:hi], xs.at[:, lo:hi], load_sem.at[g, n])
                for n, (lo, hi) in enumerate(spans)
            ]
        )
    for copies in loads:
        for copy in copies:
            copy.start()
    params = [
        pltpu.make_async_copy(src, dst, par_sem.at[s])
        for s, (src, dst) in enumerate(((w1_hbm, w1s), (w2_hbm, w2s), (b1_hbm, b1s), (b2_hbm, b2s)))
    ]
    for copy in params:
        copy.start()

    barrier = pltpu.get_barrier_semaphore()
    to_cs = [lax.rem(c + k, n_cols) for k in range(n_cols)]

    def device(to_r, to_c):
        return {"model": to_r, "cols": to_c}

    to_rs = [lax.rem(r + k, n_rows) for k in range(n_rows)]
    for kr, kc in sorted(
        ((kr, kc) for kr in range(n_rows) for kc in range(n_cols) if kr or kc),
        key=lambda k: (not (k[0] in (2, 3) and k[1] == 1), -(min(k[0], n_rows - k[0]) // 2 + min(k[1], n_cols - k[1]))),
    ):
        pl.semaphore_signal(barrier, inc=1, device_id=device(to_rs[kr], to_cs[kc]), device_id_type=MESH)

    def pack_rows(x, lo, hi):
        rows = hi - lo
        left, right = (xs[x, lo:hi, :, p].reshape(rows * pairs * 2, images) for p in range(2))
        both = jnp.concatenate([left, right], axis=1)
        packed[pl.ds(chip_h * x + lo, rows)] = both.reshape(rows, pairs, 2, 2 * images)

    def pack(g):
        for copy in loads[g]:
            copy.wait()

        def body(x, carry):
            for lo, hi in groups[g]:
                pack_rows(x, lo, hi)
            return carry

        lax.fori_loop(0, n_rows // 2, body, 0)

    last = tile_h + 4

    def rows_of(offset, count):
        def where(to_r):
            q = lax.rem(to_r, 2)
            src = tile_h * to_r + offset + (tile_h - count - 2 * offset) * q
            dst = offset + 2 + (last - count - 2 * offset - 3) * q
            return src, dst

        return where

    chunks = (
        (FIRST_ROWS, rows_of(near, FIRST_ROWS), False),
        *((2, rows_of(k, 2), False) for k in range(near - 2, -1, -2)),
        (2, rows_of(-2, 2), True),
    )
    no_outer = (r == 0) | (r == n_rows - 1)
    at_edge = (c == 0) | (c == n_cols - 1)
    own_j = c == 0
    own_j = own_j.astype(jnp.int32)

    def send_tile(chunk, to_r, to_c, there):
        rows, where, is_outer = chunks[chunk]
        src, dst = where(to_r)
        skip = (to_c == 0).astype(jnp.int32)
        edge = (to_c == 0) | (to_c == n_cols - 1)
        if is_outer:
            there = there & (to_r > 0) & (to_r < n_rows - 1)

        def copy(count, src_j, dst_j):
            pltpu.make_async_remote_copy(
                src_ref=packed.at[pl.ds(src, rows), pl.ds(src_j, count)],
                dst_ref=recv.at[me, pl.ds(dst, rows), pl.ds(dst_j, count)],
                send_sem=send_sem.at[chunk],
                recv_sem=recv_sem.at[chunk],
                device_id=device(to_r, to_c),
                device_id_type=MESH,
            ).start()

        pl.when(there & edge)(lambda: copy(win_j - 1, tile_j * to_c - 1 + skip, skip))
        pl.when(there & jnp.logical_not(edge))(lambda: copy(win_j, tile_j * to_c - 1, 0))

    chips = n_rows // 2
    ahead_r, ahead_c = AHEAD

    def step(t, table):
        value = jnp.int32(table[-1])
        for k, entry in enumerate(table[:-1]):
            value = jnp.where(t == k, entry, value)
        return value

    def turn_to(t):
        dx = step(t, CHIPS_ALONG)
        return lax.rem(r // 2 + dx, chips), dx

    def send_chip(chunk, t, rest, where=None):
        x, dx = turn_to(t)
        way = 1 - 2 * lax.rem(par + t, 2)
        for other, dy in CHIP_ORDER:
            to_r = 2 * x + (1 - par if other else par)
            to_c = lax.rem(c + way * dy + n_cols, n_cols)
            there = True
            if not other and dy == 0:
                there = dx > 0
            if rest:
                there = there & jnp.logical_not((to_r == ahead_r) & (to_c == ahead_c))
            if where is not None:
                there = there & where(to_c)
            send_tile(chunk, to_r, to_c, there)

    def send_ahead(chunk):
        send_tile(chunk, jnp.int32(ahead_r), jnp.int32(ahead_c), (r != ahead_r) | (c != ahead_c))

    def send_chunk(chunk):

        def first_column(t, carry):
            x, _ = turn_to(t)
            for other in range(2):
                to_r = 2 * x + (1 - par if other else par)
                there = ((to_r != r) | (c != 0)) & (to_r != ahead_r)
                send_tile(chunk, to_r, jnp.int32(0), there)
            return carry

        where = None
        if chunk in COLUMN_FIRST:
            lax.fori_loop(0, chips, first_column, 0)
            where = lambda to_c: to_c > 0

        def body(t, carry):
            send_chip(chunk, t, chunk > 1, where)
            return carry

        lax.fori_loop(0, chips, body, 0)

    params[0].wait()
    for dw in range(3):
        w1own[dw] = jnp.concatenate([w1s[1, dw], w1s[0, dw]], axis=1)
    w1own[3] = jnp.concatenate([w1s[2, 0], w1s[2, 1]], axis=1)
    w1own[4] = jnp.concatenate([w1s[2, 2], jnp.zeros_like(w1s[2, 2])], axis=1)
    w1all[r // 2, par, c] = w1own[...]

    for copy in loads[0]:
        copy.wait()
    pack_rows(turn_to(0)[0], *groups[0][0])
    pl.semaphore_wait(barrier, sources - 1)

    def send_weights():
        for kr in range(0, n_rows, 2):
            for kc in range(n_cols):
                if kr or kc:
                    pltpu.make_async_remote_copy(
                        src_ref=w1own,
                        dst_ref=w1all.at[r // 2, par, c],
                        send_sem=wsend_sem,
                        recv_sem=wrecv_sem,
                        device_id=device(to_rs[kr], to_cs[kc]),
                        device_id_type=MESH,
                    ).start()

    def pack_and_send(t, carry):
        pl.when(t < chips - 1)(lambda: pack_rows(turn_to(t + 1)[0], *groups[0][0]))
        send_chip(0, t, False)
        pl.when(t == 0)(send_weights)
        return carry

    lax.fori_loop(0, chips, pack_and_send, 0)

    pack(1)
    send_chunk(1)
    pack(2)
    send_ahead(2)
    send_ahead(3)
    send_chunk(2)
    send_chunk(3)

    def own_rows(chunk):
        rows, where, _ = chunks[chunk]
        src, dst = where(r)

        def copy(count, src_j, dst_j):
            for h in range(rows):
                recv[me, dst + h, pl.ds(dst_j, count)] = packed[src + h, pl.ds(src_j, count)]

        pl.when(at_edge)(lambda: copy(win_j - 1, tile_j * c - 1 + own_j, own_j))
        pl.when(jnp.logical_not(at_edge))(lambda: copy(win_j, tile_j * c - 1, 0))

    for chunk in range(3):
        own_rows(chunk)
    pl.when(jnp.logical_not(no_outer))(lambda: own_rows(3))

    zero_row = jnp.zeros((win_j, 2, 2 * images), BF16)
    zero_col = jnp.zeros((tile_h + 2, 2, 2 * images), BF16)

    def clear(s, carry):
        recv[s, last * (1 - par)] = zero_row
        return carry

    def clear_outer(s, carry):
        recv[s, (last - 1) * par] = zero_row
        recv[s, (last - 1) * par + 1] = zero_row
        return carry

    def clear_edge(s, carry):
        recv[s, pl.ds(3 * par, tile_h + 2), (win_j - 1) * (1 - own_j)] = zero_col
        return carry

    lax.fori_loop(0, sources, clear, 0)
    pl.when(no_outer)(lambda: (lax.fori_loop(0, sources, clear_outer, 0), None)[1])
    pl.when(at_edge)(lambda: (lax.fori_loop(0, sources, clear_edge, 0), None)[1])

    low = lax.broadcasted_iota(jnp.int32, (chans, 2 * chans), 1) < chans

    def spread(wt, u, v, dw):
        ur, vr = pltpu.roll(u, chans, 1), pltpu.roll(v, chans, 1)
        zero = jnp.zeros_like(u)
        tiles = (jnp.where(low, ur, zero), u, jnp.where(low, v, ur), jnp.where(low, zero, vr))
        for k, tile in enumerate(tiles):
            tile = tile.astype(BF16)
            for b in range(2):
                wt[dw + b, k * chans : (k + 1) * chans, b * 2 * chans : (b + 1) * 2 * chans] = tile

    def blank(wt):
        zero = jnp.zeros((4 * chans, 2 * chans), BF16)
        wt[3, :, 0 : 2 * chans] = zero
        wt[0, :, 2 * chans : 4 * chans] = zero

    for copy in params[1:]:
        copy.wait()
    blank(wt1)
    blank(wt2)
    for dw in range(3):
        w = [w2s[dh, dw].astype(F32) for dh in range(3)]
        spread(
            wt2,
            jnp.concatenate([w[1], w[0]], axis=1),
            jnp.concatenate([w[2], jnp.zeros_like(w[2])], axis=1),
            dw,
        )
    bias1[...] = jnp.concatenate([b1s[...]] * 4, axis=1)
    bias2[...] = jnp.concatenate([b2s[...]] * 4, axis=1)

    def wait_bytes(ref, sem):
        pltpu.make_async_copy(ref, ref, sem).wait()

    w1_bytes = recv.at[0 : sources // 2 - 1, 0, 0:5]
    wait_bytes(w1_bytes, wrecv_sem)
    wait_bytes(w1_bytes, wsend_sem)
    partner = device(r + 1 - 2 * par, c)
    w_swap = pltpu.make_async_remote_copy(
        src_ref=w1all.at[:, par],
        dst_ref=w1all.at[:, par],
        send_sem=wswap_send_sem,
        recv_sem=wswap_recv_sem,
        device_id=partner,
        device_id_type=MESH,
    )
    w_swap.start()

    def arrived(chunk):
        def wait(count):
            wait_bytes(recv.at[0 : sources - 1, 0 : chunks[chunk][0], 0:count], recv_sem.at[chunk])

        pl.when(at_edge)(lambda: wait(win_j - 1))
        pl.when(jnp.logical_not(at_edge))(lambda: wait(win_j))

    arrived(0)
    give = tile_h - (tile_h - 3) * par
    land = tile_h + 2 - (tile_h + 1) * (1 - par)
    swap = pltpu.make_async_remote_copy(
        src_ref=recv.at[:, pl.ds(give, 2)],
        dst_ref=recv.at[:, pl.ds(land, 2)],
        send_sem=swap_send_sem,
        recv_sem=swap_recv_sem,
        device_id=partner,
        device_id_type=MESH,
    )
    swap.start()

    w_swap.wait()
    u = [w1all[:, :, :, k].reshape(chans, 2 * chans).astype(F32) for k in range(5)]
    for dw in range(3):
        v = (u[3], pltpu.roll(u[3], chans, 1), u[4])[dw]
        spread(wt1, u[dw], jnp.where(low, v, 0.0), dw)

    x_pairs, z_pairs = xmat.shape[0], ymat.shape[0]
    o_pairs = z_pairs - 1

    def nth(n, count):
        return (count - 1) * (1 - par) + n * (2 * par - 1)

    def turn_one(n, carry):
        i = nth(n, x_pairs)

        def put(j, value):
            xmat[i, j] = value

        turn(recv, i, put)
        return carry

    def first_one(n, carry):
        i = nth(n, z_pairs)
        fill = jnp.where(n == 0, 1 - par, 2)
        out_of = jnp.where(n == z_pairs - 1, jnp.where(r == 0, 0, jnp.where(r == n_rows - 1, 1, 2)), 2)
        blank_a = jnp.where(fill < 2, fill, out_of)
        first((xmat.at[i], xmat.at[i + 1]), lambda dw: wt1[dw], bias1[...], ymat.at[i], blank_a)
        return carry

    def second_one(n, carry):
        i = nth(n, o_pairs)
        second((ymat.at[i], ymat.at[i + 1]), lambda dw: wt2[dw], bias2[...], out.at[pl.ds(2 * i, 2)])
        return carry

    def stage(s, carry):
        @pl.when(s == 0)
        def _():
            swap.wait()

        for k in range(1, 4):
            there = s == k
            if k == 3:
                there = there & jnp.logical_not(no_outer)
            pl.when(there)(lambda k=k: arrived(k))

        later = (s + 3) // 4
        lax.fori_loop((2 + s) * later, 3 + s, turn_one, 0)
        lax.fori_loop((1 + s) * later, 2 + s, first_one, 0)
        lax.fori_loop(s, 1 + s - s // 3, second_one, 0)
        return carry

    lax.fori_loop(0, 4, stage, 0)

    per_edge = n_rows * 2
    for chunk in range(4):
        rows = chunks[chunk][0]
        n_r = n_rows - 2 if chunk == 3 else n_rows
        counts = (n_r * 2, n_r * (n_cols - 2))

        def drain(edge_n, inner_n, rows=rows, chunk=chunk):
            wait_bytes(recv.at[0:edge_n, 0:rows, 0 : win_j - 1], send_sem.at[chunk])
            wait_bytes(recv.at[0:inner_n, 0:rows, 0:win_j], send_sem.at[chunk])

        def drain_own(chunk=chunk, counts=counts, drain=drain):
            pl.when(at_edge)(lambda: drain(counts[0] - 1, counts[1]))
            pl.when(jnp.logical_not(at_edge))(lambda: drain(counts[0], counts[1] - 1))

        if chunk == 3:
            pl.when(no_outer)(lambda: drain(*counts))
            pl.when(jnp.logical_not(no_outer))(drain_own)
        else:
            drain_own()


def tail_kernel(tile, ymat, wt2, bias2, out_hbm, o_new, sem):
    par = lax.rem(lax.axis_index("model"), 2)
    rows = out_hbm.shape[0]
    o_pairs = ymat.shape[0] - 1
    late = (rows - 2) * par
    here = 2 * (1 - par)

    def start(k, carry):
        pltpu.make_async_copy(tile.at[par + k], out_hbm.at[k], sem.at[0]).start()
        return carry

    lax.fori_loop(here, here + rows - 2, start, 0)
    i = (o_pairs - 1) * par
    second((ymat.at[i], ymat.at[i + 1]), lambda dw: wt2[dw], bias2[...], o_new)
    last = pltpu.make_async_copy(o_new, out_hbm.at[pl.ds(late, 2)], sem.at[1])
    last.start()
    pltpu.make_async_copy(tile.at[0 : rows - 2], out_hbm.at[0 : rows - 2], sem.at[0]).wait()
    last.wait()


def solution(mesh):
    n_rows = mesh.shape["model"]
    n_cols = mesh.shape["cols"]

    def run_local(x_in, w_conv1, b_conv1, w_conv2, b_conv2):
        images, height, width, own_chans = x_in.shape
        sources = n_rows * n_cols
        chans = own_chans * sources
        pairs = width // 2
        tile_h, tile_j = height // n_rows, pairs // n_cols
        win_j = tile_j + 2
        x_pairs, z_pairs = (tile_h + 5) // 2, (tile_h + 3) // 2
        x_t = jnp.transpose(x_in, (1, 2, 3, 0)).reshape(n_rows // 2, 2 * tile_h, pairs, 2, own_chans, images)
        args = (x_t, w_conv1, b_conv1.reshape(1, chans), w_conv2, b_conv2.reshape(1, chans))
        hbm = pl.BlockSpec(memory_space=pltpu.HBM)
        vmem = pl.BlockSpec(memory_space=pltpu.VMEM)
        kept = (
            pltpu.VMEM((2 * (z_pairs - 1), tile_j, 2, images, chans), F32),
            pltpu.VMEM((z_pairs, win_j - 1, 2, images, 2 * chans), BF16),
            pltpu.VMEM((4, 4 * chans, 4 * chans), BF16),
            pltpu.VMEM((1, 4 * chans), F32),
        )
        state = pl.pallas_call(
            functools.partial(conv_kernel, n_rows, n_cols),
            out_shape=kept,
            in_specs=[hbm] * 5,
            out_specs=[vmem] * len(kept),
            scratch_shapes=[
                pltpu.VMEM((sources, 2 * x_pairs, win_j, own_chans, 2 * images), BF16),
                pltpu.VMEM((x_pairs, win_j, 2, images, 2 * chans), BF16),
                pltpu.VMEM((4, 4 * chans, 4 * chans), BF16),
                pltpu.VMEM((1, 4 * chans), F32),
                pltpu.VMEM((n_rows // 2, 2 * tile_h, pairs, 2, own_chans, images), BF16),
                pltpu.VMEM((height, pairs, own_chans, 2 * images), BF16),
                pltpu.VMEM((3, 3, own_chans, chans), BF16),
                pltpu.VMEM((5, own_chans, 2 * chans), BF16),
                pltpu.VMEM((n_rows // 2, 2, n_cols, 5, own_chans, 2 * chans), BF16),
                pltpu.VMEM((3, 3, chans, chans), BF16),
                pltpu.VMEM((1, chans), F32),
                pltpu.VMEM((1, chans), F32),
                pltpu.SemaphoreType.DMA((3, 2)),
                pltpu.SemaphoreType.DMA((4,)),
                pltpu.SemaphoreType.DMA((4,)),
                pltpu.SemaphoreType.DMA((4,)),
            ]
            + [pltpu.SemaphoreType.DMA] * 6,
            compiler_params=pltpu.CompilerParams(
                collective_id=0, has_side_effects=True, vmem_limit_bytes=24 << 20
            ),
            name="conv",
        )(*(pltpu.with_memory_space_constraint(a, pltpu.HBM) for a in args))
        out = pl.pallas_call(
            tail_kernel,
            out_shape=jax.ShapeDtypeStruct((tile_h, tile_j, 2, images, chans), F32),
            in_specs=[vmem] * len(kept),
            out_specs=pl.BlockSpec(memory_space=pl.ANY),
            scratch_shapes=[
                pltpu.VMEM((2, tile_j, 2, images, chans), F32),
                pltpu.SemaphoreType.DMA((2,)),
            ],
            compiler_params=pltpu.CompilerParams(vmem_limit_bytes=8 << 20),
            name="tail",
        )(*state)
        out = out.reshape(tile_h, 2 * tile_j, images, chans)
        return jnp.transpose(out, (2, 0, 1, 3))

    group = ("model", "cols")
    return jax.shard_map(
        run_local,
        mesh=mesh,
        in_specs=(P("data", None, None, group), P(None, None, group, None), P(), P(), P()),
        out_specs=P("data", "model", "cols", None),
        check_vma=False,
    )
```

time: 914 us -> 26.2 us (0.03)
  the two profiles are of different devices: /device:TPU:97 before, /device:TPU:99 now
where the time goes in v1:
time: 26.2 us; the launch traced here: 26.1 us
  Pallas kernels  26.1 us (100%)
    pallas_call x1, Pallas kernels, run_local(): pl.pallas_call(functools.partial(conv_kernel, n_rows, n_cols), out_shape=...  24.4 us
    pallas_call x1, Pallas kernels, run_local(): pl.pallas_call(tail_kernel, out_shape=jax.ShapeDtypeStruct((tile_h, tile_...  1.71 us

profile of v1, /device:TPU:99, one launch (start us, length us, event | category | flops | bytes accessed | tf_op | source)
XLA Modules:
  0.0 26.1 jit_solution(14931458964200887930)
XLA Ops:
  0.0 24.4 %conv.1 = (f32[8,7,2,64,64]{4,3,2,1,0:T(8,128)S(1)}, bf16[5,8,2,64,128]{4,3,2,1,0:T(8,128)(2,1)S(1)}, bf16[4,256,256]{2,1,0:T(8,128)(2,1)S(1)}, f32[1,256]{1,0:T(1,128)S(1)}) custom-call(bf16[4,14,28,2,2,64]{5,4,3,2,1,0:T(2,128)(2,1)} %bitcast.8, bf16[3,3,2,64]{3,2,1,0:T(2,128)(2,1)} %w1_hbm.1, f32[1,64]{1,0:T(1,128)} %bitcast.9, ...), custom_call_target="tpu_custom_call" | custom-call | tf_op jit(solution)/shard_map/conv/pallas_call | solution.py:516
  24.4 1.7 %tail.1 = f32[7,7,2,64,64]{4,3,2,1,0:T(8,128)} custom-call(f32[8,7,2,64,64]{4,3,2,1,0:T(8,128)S(1)} %get-tuple-element.9.tile, bf16[5,8,2,64,128]{4,3,2,1,0:T(8,128)(2,1)S(1)} %get-tuple-element.10.ymat, bf16[4,256,256]{2,1,0:T(8,128)(2,1)S(1)} %get-tuple-element.11.wt2, f32[1,256]{1,0:T(1,128)S(1)} %get-tuple-element.12.bias2), custom_call_target="tpu_custom_call" | custom-call | tf_op jit(solution)/shard_map/tail/pallas_call | solution.py:545

commit v2 on v1

--- a/solution.py
+++ b/solution.py
@@ -13,7 +13,7 @@
 FIRST_ROWS = 3
 AHEAD = (1, 0)
 COLUMN_FIRST = (2, 3)
-CHIPS_ALONG = (1, 3, 2, 0)
+CHIPS_ALONG = (3, 1, 2, 0)
 CHIP_ORDER = tuple((other, dy) for other in (0, 1) for dy in (1, -1, 0, 2))
 
 
@@ -248,7 +248,7 @@
             where = lambda to_c: to_c > 0
 
         def body(t, carry):
-            send_chip(chunk, t, chunk > 1, where)
+            send_chip(chunk, t, True, where)
             return carry
 
         lax.fori_loop(0, chips, body, 0)
@@ -287,6 +287,7 @@
     lax.fori_loop(0, chips, pack_and_send, 0)
 
     pack(1)
+    send_ahead(1)
     send_chunk(1)
     pack(2)
     send_ahead(2)

time: 26.2 us -> 25.9 us (0.989)
  the two profiles are of different devices: /device:TPU:99 before, /device:TPU:97 now
where the time goes in v2:
time: 25.9 us
  Pallas kernels  25.8 us (100%)
    pallas_call x1, Pallas kernels, run_local(): pl.pallas_call(functools.partial(conv_kernel, n_rows, n_cols), out_shape=...  24.1 us
    pallas_call x1, Pallas kernels, run_local(): pl.pallas_call(tail_kernel, out_shape=jax.ShapeDtypeStruct((tile_h, tile_...  1.71 us

profile of v2, /device:TPU:97, one launch (start us, length us, event | category | flops | bytes accessed | tf_op | source)
XLA Modules:
  0.0 25.9 jit_solution(9535652994503669345)
XLA Ops:
  0.0 24.1 %conv.1 = (f32[8,7,2,64,64]{4,3,2,1,0:T(8,128)S(1)}, bf16[5,8,2,64,128]{4,3,2,1,0:T(8,128)(2,1)S(1)}, bf16[4,256,256]{2,1,0:T(8,128)(2,1)S(1)}, f32[1,256]{1,0:T(1,128)S(1)}) custom-call(bf16[4,14,28,2,2,64]{5,4,3,2,1,0:T(2,128)(2,1)} %bitcast.8, bf16[3,3,2,64]{3,2,1,0:T(2,128)(2,1)} %w1_hbm.1, f32[1,64]{1,0:T(1,128)} %bitcast.9, ...), custom_call_target="tpu_custom_call" | custom-call | tf_op jit(solution)/shard_map/conv/pallas_call | solution.py:517
  24.1 1.7 %tail.1 = f32[7,7,2,64,64]{4,3,2,1,0:T(8,128)} custom-call(f32[8,7,2,64,64]{4,3,2,1,0:T(8,128)S(1)} %get-tuple-element.9.tile, bf16[5,8,2,64,128]{4,3,2,1,0:T(8,128)(2,1)S(1)} %get-tuple-element.10.ymat, bf16[4,256,256]{2,1,0:T(8,128)(2,1)S(1)} %get-tuple-element.11.wt2, f32[1,256]{1,0:T(1,128)S(1)} %get-tuple-element.12.bias2), custom_call_target="tpu_custom_call" | custom-call | tf_op jit(solution)/shard_map/tail/pallas_call | solution.py:546

commit v3 on v2

--- a/solution.py
+++ b/solution.py
@@ -13,7 +13,7 @@
 FIRST_ROWS = 3
 AHEAD = (1, 0)
 COLUMN_FIRST = (2, 3)
-CHIPS_ALONG = (3, 1, 2, 0)
+CHIPS_ALONG = (1, 3, 2, 0)
 CHIP_ORDER = tuple((other, dy) for other in (0, 1) for dy in (1, -1, 0, 2))
 
 
@@ -216,7 +216,7 @@
 
     def send_chip(chunk, t, rest, where=None):
         x, dx = turn_to(t)
-        way = 1 - 2 * lax.rem(par + t, 2)
+        way = 1 - 2 * par
         for other, dy in CHIP_ORDER:
             to_r = 2 * x + (1 - par if other else par)
             to_c = lax.rem(c + way * dy + n_cols, n_cols)

time: 25.9 us -> 26.1 us (level)
  no operation moved by 1% of the time
where the time goes in v3:
time: 26.1 us; the launch traced here: 26 us
  Pallas kernels  26 us (100%)
    pallas_call x1, Pallas kernels, run_local(): pl.pallas_call(functools.partial(conv_kernel, n_rows, n_cols), out_shape=...  24.3 us
    pallas_call x1, Pallas kernels, run_local(): pl.pallas_call(tail_kernel, out_shape=jax.ShapeDtypeStruct((tile_h, tile_...  1.71 us

profile of v3, /device:TPU:97, one launch (start us, length us, event | category | flops | bytes accessed | tf_op | source)
XLA Modules:
  0.0 26.0 jit_solution(6275444998009937739)
XLA Ops:
  0.0 24.3 %conv.1 = (f32[8,7,2,64,64]{4,3,2,1,0:T(8,128)S(1)}, bf16[5,8,2,64,128]{4,3,2,1,0:T(8,128)(2,1)S(1)}, bf16[4,256,256]{2,1,0:T(8,128)(2,1)S(1)}, f32[1,256]{1,0:T(1,128)S(1)}) custom-call(bf16[4,14,28,2,2,64]{5,4,3,2,1,0:T(2,128)(2,1)} %bitcast.8, bf16[3,3,2,64]{3,2,1,0:T(2,128)(2,1)} %w1_hbm.1, f32[1,64]{1,0:T(1,128)} %bitcast.9, ...), custom_call_target="tpu_custom_call" | custom-call | tf_op jit(solution)/shard_map/conv/pallas_call | solution.py:517
  24.3 1.7 %tail.1 = f32[7,7,2,64,64]{4,3,2,1,0:T(8,128)} custom-call(f32[8,7,2,64,64]{4,3,2,1,0:T(8,128)S(1)} %get-tuple-element.9.tile, bf16[5,8,2,64,128]{4,3,2,1,0:T(8,128)(2,1)S(1)} %get-tuple-element.10.ymat, bf16[4,256,256]{2,1,0:T(8,128)(2,1)S(1)} %get-tuple-element.11.wt2, f32[1,256]{1,0:T(1,128)S(1)} %get-tuple-element.12.bias2), custom_call_target="tpu_custom_call" | custom-call | tf_op jit(solution)/shard_map/tail/pallas_call | solution.py:546

commit v4 on v2

--- a/solution.py
+++ b/solution.py
@@ -10,7 +10,8 @@
 MESH = pl.DeviceIdType.MESH
 BF16 = jnp.bfloat16
 F32 = jnp.float32
-FIRST_ROWS = 3
+CHUNK_ROWS = (2, 3, 2)
+TURNS, FIRSTS, SECONDS = (2, 4, 5, 6), (1, 3, 4, 5), (0, 2, 3, 3)
 AHEAD = (1, 0)
 COLUMN_FIRST = (2, 3)
 CHIPS_ALONG = (3, 1, 2, 0)
@@ -109,8 +110,11 @@
     me = r * n_cols + c
     chans = recv.shape[0] * 2
 
-    near = tile_h - FIRST_ROWS
-    groups = (((near, chip_h - near),), *(((k, k + 2), (chip_h - k - 2, chip_h - k)) for k in range(near - 2, -1, -2)))
+    tops = [tile_h - sum(CHUNK_ROWS[: k + 1]) for k in range(len(CHUNK_ROWS))]
+    groups = (
+        ((tops[0], chip_h - tops[0]),),
+        *(((k, k + n), (chip_h - k - n, chip_h - k)) for k, n in zip(tops[1:], CHUNK_ROWS[1:])),
+    )
     loads = []
     for g, spans in enumerate(groups):
         loads.append(
@@ -171,8 +175,7 @@
         return where
 
     chunks = (
-        (FIRST_ROWS, rows_of(near, FIRST_ROWS), False),
-        *((2, rows_of(k, 2), False) for k in range(near - 2, -1, -2)),
+        *((n, rows_of(k, n), False) for k, n in zip(tops, CHUNK_ROWS)),
         (2, rows_of(-2, 2), True),
     )
     no_outer = (r == 0) | (r == n_rows - 1)
@@ -443,10 +446,8 @@
                 there = there & jnp.logical_not(no_outer)
             pl.when(there)(lambda k=k: arrived(k))
 
-        later = (s + 3) // 4
-        lax.fori_loop((2 + s) * later, 3 + s, turn_one, 0)
-        lax.fori_loop((1 + s) * later, 2 + s, first_one, 0)
-        lax.fori_loop(s, 1 + s - s // 3, second_one, 0)
+        for ends, one in ((TURNS, turn_one), (FIRSTS, first_one), (SECONDS, second_one)):
+            lax.fori_loop(step(s, (0, *ends[:-1])), step(s, ends), one, 0)
         return carry
 
     lax.fori_loop(0, 4, stage, 0)

time: 25.9 us -> 25.7 us (level)
  no operation moved by 1% of the time
where the time goes in v4:
time: 25.7 us; the launch traced here: 25.6 us
  Pallas kernels  25.6 us (100%)
    pallas_call x1, Pallas kernels, run_local(): pl.pallas_call(functools.partial(conv_kernel, n_rows, n_cols), out_shape=...  23.9 us
    pallas_call x1, Pallas kernels, run_local(): pl.pallas_call(tail_kernel, out_shape=jax.ShapeDtypeStruct((tile_h, tile_...  1.71 us

profile of v4, /device:TPU:97, one launch (start us, length us, event | category | flops | bytes accessed | tf_op | source)
XLA Modules:
  0.0 25.6 jit_solution(9308061783278636343)
XLA Ops:
  0.0 23.9 %conv.1 = (f32[8,7,2,64,64]{4,3,2,1,0:T(8,128)S(1)}, bf16[5,8,2,64,128]{4,3,2,1,0:T(8,128)(2,1)S(1)}, bf16[4,256,256]{2,1,0:T(8,128)(2,1)S(1)}, f32[1,256]{1,0:T(1,128)S(1)}) custom-call(bf16[4,14,28,2,2,64]{5,4,3,2,1,0:T(2,128)(2,1)} %bitcast.8, bf16[3,3,2,64]{3,2,1,0:T(2,128)(2,1)} %w1_hbm.1, f32[1,64]{1,0:T(1,128)} %bitcast.9, ...), custom_call_target="tpu_custom_call" | custom-call | tf_op jit(solution)/shard_map/conv/pallas_call | solution.py:518
  23.9 1.7 %tail.1 = f32[7,7,2,64,64]{4,3,2,1,0:T(8,128)} custom-call(f32[8,7,2,64,64]{4,3,2,1,0:T(8,128)S(1)} %get-tuple-element.9.tile, bf16[5,8,2,64,128]{4,3,2,1,0:T(8,128)(2,1)S(1)} %get-tuple-element.10.ymat, bf16[4,256,256]{2,1,0:T(8,128)(2,1)S(1)} %get-tuple-element.11.wt2, f32[1,256]{1,0:T(1,128)S(1)} %get-tuple-element.12.bias2), custom_call_target="tpu_custom_call" | custom-call | tf_op jit(solution)/shard_map/tail/pallas_call | solution.py:547

commit v5 on v4

--- a/solution.py
+++ b/solution.py
@@ -219,7 +219,7 @@
 
     def send_chip(chunk, t, rest, where=None):
         x, dx = turn_to(t)
-        way = 1 - 2 * lax.rem(par + t, 2)
+        way = 1 - 2 * par
         for other, dy in CHIP_ORDER:
             to_r = 2 * x + (1 - par if other else par)
             to_c = lax.rem(c + way * dy + n_cols, n_cols)

time: 25.7 us -> 26.7 us (1.039)
  the two profiles are of different devices: /device:TPU:97 before, /device:TPU:99 now
where the time goes in v5:
time: 26.7 us; the launch traced here: 26.6 us
  Pallas kernels  26.6 us (100%)
    pallas_call x1, Pallas kernels, run_local(): pl.pallas_call(functools.partial(conv_kernel, n_rows, n_cols), out_shape=...  24.9 us
    pallas_call x1, Pallas kernels, run_local(): pl.pallas_call(tail_kernel, out_shape=jax.ShapeDtypeStruct((tile_h, tile_...  1.71 us

profile of v5, /device:TPU:99, one launch (start us, length us, event | category | flops | bytes accessed | tf_op | source)
XLA Modules:
  0.0 26.6 jit_solution(1477350087916499623)
XLA Ops:
  0.0 24.9 %conv.1 = (f32[8,7,2,64,64]{4,3,2,1,0:T(8,128)S(1)}, bf16[5,8,2,64,128]{4,3,2,1,0:T(8,128)(2,1)S(1)}, bf16[4,256,256]{2,1,0:T(8,128)(2,1)S(1)}, f32[1,256]{1,0:T(1,128)S(1)}) custom-call(bf16[4,14,28,2,2,64]{5,4,3,2,1,0:T(2,128)(2,1)} %bitcast.8, bf16[3,3,2,64]{3,2,1,0:T(2,128)(2,1)} %w1_hbm.1, f32[1,64]{1,0:T(1,128)} %bitcast.9, ...), custom_call_target="tpu_custom_call" | custom-call | tf_op jit(solution)/shard_map/conv/pallas_call | solution.py:518
  24.9 1.7 %tail.1 = f32[7,7,2,64,64]{4,3,2,1,0:T(8,128)} custom-call(f32[8,7,2,64,64]{4,3,2,1,0:T(8,128)S(1)} %get-tuple-element.9.tile, bf16[5,8,2,64,128]{4,3,2,1,0:T(8,128)(2,1)S(1)} %get-tuple-element.10.ymat, bf16[4,256,256]{2,1,0:T(8,128)(2,1)S(1)} %get-tuple-element.11.wt2, f32[1,256]{1,0:T(1,128)S(1)} %get-tuple-element.12.bias2), custom_call_target="tpu_custom_call" | custom-call | tf_op jit(solution)/shard_map/tail/pallas_call | solution.py:547

commit v6 on v4

--- a/solution.py
+++ b/solution.py
@@ -290,13 +290,30 @@
     lax.fori_loop(0, chips, pack_and_send, 0)
 
     pack(1)
+    pack(2)
     send_ahead(1)
+    send_ahead(2)
     send_chunk(1)
-    pack(2)
-    send_ahead(2)
     send_ahead(3)
     send_chunk(2)
     send_chunk(3)
+
+    def wait_bytes(ref, sem):
+        pltpu.make_async_copy(ref, ref, sem).wait()
+
+    w1_bytes = recv.at[0 : sources // 2 - 1, 0, 0:5]
+    wait_bytes(w1_bytes, wrecv_sem)
+    wait_bytes(w1_bytes, wsend_sem)
+    partner = device(r + 1 - 2 * par, c)
+    w_swap = pltpu.make_async_remote_copy(
+        src_ref=w1all.at[:, par],
+        dst_ref=w1all.at[:, par],
+        send_sem=wswap_send_sem,
+        recv_sem=wswap_recv_sem,
+        device_id=partner,
+        device_id_type=MESH,
+    )
+    w_swap.start()
 
     def own_rows(chunk):
         rows, where, _ = chunks[chunk]
@@ -363,23 +380,6 @@
         )
     bias1[...] = jnp.concatenate([b1s[...]] * 4, axis=1)
     bias2[...] = jnp.concatenate([b2s[...]] * 4, axis=1)
-
-    def wait_bytes(ref, sem):
-        pltpu.make_async_copy(ref, ref, sem).wait()
-
-    w1_bytes = recv.at[0 : sources // 2 - 1, 0, 0:5]
-    wait_bytes(w1_bytes, wrecv_sem)
-    wait_bytes(w1_bytes, wsend_sem)
-    partner = device(r + 1 - 2 * par, c)
-    w_swap = pltpu.make_async_remote_copy(
-        src_ref=w1all.at[:, par],
-        dst_ref=w1all.at[:, par],
-        send_sem=wswap_send_sem,
-        recv_sem=wswap_recv_sem,
-        device_id=partner,
-        device_id_type=MESH,
-    )
-    w_swap.start()
 
     def arrived(chunk):
         def wait(count):

time: 25.7 us -> 27.1 us (1.054)
  the two profiles are of different devices: /device:TPU:97 before, /device:TPU:101 now
where the time goes in v6:
time: 27.1 us
  Pallas kernels  27 us (100%)
    pallas_call x1, Pallas kernels, run_local(): pl.pallas_call(functools.partial(conv_kernel, n_rows, n_cols), out_shape=...  25.3 us
    pallas_call x1, Pallas kernels, run_local(): pl.pallas_call(tail_kernel, out_shape=jax.ShapeDtypeStruct((tile_h, tile_...  1.71 us

profile of v6, /device:TPU:101, one launch (start us, length us, event | category | flops | bytes accessed | tf_op | source)
XLA Modules:
  0.0 27.1 jit_solution(1705962213018645193)
XLA Ops:
  0.0 25.3 %conv.1 = (f32[8,7,2,64,64]{4,3,2,1,0:T(8,128)S(1)}, bf16[5,8,2,64,128]{4,3,2,1,0:T(8,128)(2,1)S(1)}, bf16[4,256,256]{2,1,0:T(8,128)(2,1)S(1)}, f32[1,256]{1,0:T(1,128)S(1)}) custom-call(bf16[4,14,28,2,2,64]{5,4,3,2,1,0:T(2,128)(2,1)} %bitcast.8, bf16[3,3,2,64]{3,2,1,0:T(2,128)(2,1)} %w1_hbm.1, f32[1,64]{1,0:T(1,128)} %bitcast.9, ...), custom_call_target="tpu_custom_call" | custom-call | tf_op jit(solution)/shard_map/conv/pallas_call | solution.py:518
  25.3 1.7 %tail.1 = f32[7,7,2,64,64]{4,3,2,1,0:T(8,128)} custom-call(f32[8,7,2,64,64]{4,3,2,1,0:T(8,128)S(1)} %get-tuple-element.9.tile, bf16[5,8,2,64,128]{4,3,2,1,0:T(8,128)(2,1)S(1)} %get-tuple-element.10.ymat, bf16[4,256,256]{2,1,0:T(8,128)(2,1)S(1)} %get-tuple-element.11.wt2, f32[1,256]{1,0:T(1,128)S(1)} %get-tuple-element.12.bias2), custom_call_target="tpu_custom_call" | custom-call | tf_op jit(solution)/shard_map/tail/pallas_call | solution.py:547

commit v7 on v6

--- a/solution.py
+++ b/solution.py
@@ -290,10 +290,10 @@
     lax.fori_loop(0, chips, pack_and_send, 0)
 
     pack(1)
+    send_ahead(1)
+    send_chunk(1)
     pack(2)
-    send_ahead(1)
     send_ahead(2)
-    send_chunk(1)
     send_ahead(3)
     send_chunk(2)
     send_chunk(3)

time: 27.1 us -> 25.7 us (0.948)
  the two profiles are of different devices: /device:TPU:101 before, /device:TPU:97 now
where the time goes in v7:
time: 25.7 us; the launch traced here: 25.6 us
  Pallas kernels  25.6 us (100%)
    pallas_call x1, Pallas kernels, run_local(): pl.pallas_call(functools.partial(conv_kernel, n_rows, n_cols), out_shape=...  23.9 us
    pallas_call x1, Pallas kernels, run_local(): pl.pallas_call(tail_kernel, out_shape=jax.ShapeDtypeStruct((tile_h, tile_...  1.71 us

profile of v7, /device:TPU:97, one launch (start us, length us, event | category | flops | bytes accessed | tf_op | source)
XLA Modules:
  0.0 25.6 jit_solution(7681948131936969565)
XLA Ops:
  0.0 23.9 %conv.1 = (f32[8,7,2,64,64]{4,3,2,1,0:T(8,128)S(1)}, bf16[5,8,2,64,128]{4,3,2,1,0:T(8,128)(2,1)S(1)}, bf16[4,256,256]{2,1,0:T(8,128)(2,1)S(1)}, f32[1,256]{1,0:T(1,128)S(1)}) custom-call(bf16[4,14,28,2,2,64]{5,4,3,2,1,0:T(2,128)(2,1)} %bitcast.8, bf16[3,3,2,64]{3,2,1,0:T(2,128)(2,1)} %w1_hbm.1, f32[1,64]{1,0:T(1,128)} %bitcast.9, ...), custom_call_target="tpu_custom_call" | custom-call | tf_op jit(solution)/shard_map/conv/pallas_call | solution.py:518
  23.9 1.7 %tail.1 = f32[7,7,2,64,64]{4,3,2,1,0:T(8,128)} custom-call(f32[8,7,2,64,64]{4,3,2,1,0:T(8,128)S(1)} %get-tuple-element.9.tile, bf16[5,8,2,64,128]{4,3,2,1,0:T(8,128)(2,1)S(1)} %get-tuple-element.10.ymat, bf16[4,256,256]{2,1,0:T(8,128)(2,1)S(1)} %get-tuple-element.11.wt2, f32[1,256]{1,0:T(1,128)S(1)} %get-tuple-element.12.bias2), custom_call_target="tpu_custom_call" | custom-call | tf_op jit(solution)/shard_map/tail/pallas_call | solution.py:547

commit v8 on v7

--- a/solution.py
+++ b/solution.py
@@ -251,7 +251,7 @@
             where = lambda to_c: to_c > 0
 
         def body(t, carry):
-            send_chip(chunk, t, True, where)
+            send_chip(chunk, t, chunk > 1, where)
             return carry
 
         lax.fori_loop(0, chips, body, 0)
@@ -290,7 +290,6 @@
     lax.fori_loop(0, chips, pack_and_send, 0)
 
     pack(1)
-    send_ahead(1)
     send_chunk(1)
     pack(2)
     send_ahead(2)

time: 25.7 us -> 26.7 us (1.039)
  Pallas kernels: 25.6 us -> 26.6 us
    pallas_call x1, Pallas kernels: 23.9 us -> 24.9 us  [run_local(): pl.pallas_call(functools.partial(conv_kernel, n_rows, n_cols), out_shape=...]
where the time goes in v8:
time: 26.7 us; the launch traced here: 26.6 us
  Pallas kernels  26.6 us (100%)
    pallas_call x1, Pallas kernels, run_local(): pl.pallas_call(functools.partial(conv_kernel, n_rows, n_cols), out_shape=...  24.9 us
    pallas_call x1, Pallas kernels, run_local(): pl.pallas_call(tail_kernel, out_shape=jax.ShapeDtypeStruct((tile_h, tile_...  1.71 us

profile of v8, /device:TPU:97, one launch (start us, length us, event | category | flops | bytes accessed | tf_op | source)
XLA Modules:
  0.0 26.6 jit_solution(6951153608274373514)
XLA Ops:
  0.0 24.9 %conv.1 = (f32[8,7,2,64,64]{4,3,2,1,0:T(8,128)S(1)}, bf16[5,8,2,64,128]{4,3,2,1,0:T(8,128)(2,1)S(1)}, bf16[4,256,256]{2,1,0:T(8,128)(2,1)S(1)}, f32[1,256]{1,0:T(1,128)S(1)}) custom-call(bf16[4,14,28,2,2,64]{5,4,3,2,1,0:T(2,128)(2,1)} %bitcast.8, bf16[3,3,2,64]{3,2,1,0:T(2,128)(2,1)} %w1_hbm.1, f32[1,64]{1,0:T(1,128)} %bitcast.9, ...), custom_call_target="tpu_custom_call" | custom-call | tf_op jit(solution)/shard_map/conv/pallas_call | solution.py:517
  24.9 1.7 %tail.1 = f32[7,7,2,64,64]{4,3,2,1,0:T(8,128)} custom-call(f32[8,7,2,64,64]{4,3,2,1,0:T(8,128)S(1)} %get-tuple-element.9.tile, bf16[5,8,2,64,128]{4,3,2,1,0:T(8,128)(2,1)S(1)} %get-tuple-element.10.ymat, bf16[4,256,256]{2,1,0:T(8,128)(2,1)S(1)} %get-tuple-element.11.wt2, f32[1,256]{1,0:T(1,128)S(1)} %get-tuple-element.12.bias2), custom_call_target="tpu_custom_call" | custom-call | tf_op jit(solution)/shard_map/tail/pallas_call | solution.py:546

commit v9 on v7

--- a/solution.py
+++ b/solution.py
@@ -15,7 +15,7 @@
 AHEAD = (1, 0)
 COLUMN_FIRST = (2, 3)
 CHIPS_ALONG = (3, 1, 2, 0)
-CHIP_ORDER = tuple((other, dy) for other in (0, 1) for dy in (1, -1, 0, 2))
+CHIP_ORDER = tuple((other, dy) for other in (0, 1) for dy in (0, 1, -1, 2))
 
 
 def turn(recv, i, put):

time: 25.7 us -> 25.7 us (level); the launches traced: 25.6 us -> 25.3 us
  Pallas kernels: 25.6 us -> 25.3 us
    pallas_call x1, Pallas kernels: 23.9 us -> 23.6 us  [run_local(): pl.pallas_call(functools.partial(conv_kernel, n_rows, n_cols), out_shape=...]
where the time goes in v9:
time: 25.7 us; the launch traced here: 25.3 us
  Pallas kernels  25.3 us (98%)
    pallas_call x1, Pallas kernels, run_local(): pl.pallas_call(functools.partial(conv_kernel, n_rows, n_cols), out_shape=...  23.6 us
    pallas_call x1, Pallas kernels, run_local(): pl.pallas_call(tail_kernel, out_shape=jax.ShapeDtypeStruct((tile_h, tile_...  1.71 us

profile of v9, /device:TPU:97, one launch (start us, length us, event | category | flops | bytes accessed | tf_op | source)
XLA Modules:
  0.0 25.3 jit_solution(10404783413693383375)
XLA Ops:
  0.0 23.6 %conv.1 = (f32[8,7,2,64,64]{4,3,2,1,0:T(8,128)S(1)}, bf16[5,8,2,64,128]{4,3,2,1,0:T(8,128)(2,1)S(1)}, bf16[4,256,256]{2,1,0:T(8,128)(2,1)S(1)}, f32[1,256]{1,0:T(1,128)S(1)}) custom-call(bf16[4,14,28,2,2,64]{5,4,3,2,1,0:T(2,128)(2,1)} %bitcast.8, bf16[3,3,2,64]{3,2,1,0:T(2,128)(2,1)} %w1_hbm.1, f32[1,64]{1,0:T(1,128)} %bitcast.9, ...), custom_call_target="tpu_custom_call" | custom-call | tf_op jit(solution)/shard_map/conv/pallas_call | solution.py:518
  23.6 1.7 %tail.1 = f32[7,7,2,64,64]{4,3,2,1,0:T(8,128)} custom-call(f32[8,7,2,64,64]{4,3,2,1,0:T(8,128)S(1)} %get-tuple-element.9.tile, bf16[5,8,2,64,128]{4,3,2,1,0:T(8,128)(2,1)S(1)} %get-tuple-element.10.ymat, bf16[4,256,256]{2,1,0:T(8,128)(2,1)S(1)} %get-tuple-element.11.wt2, f32[1,256]{1,0:T(1,128)S(1)} %get-tuple-element.12.bias2), custom_call_target="tpu_custom_call" | custom-call | tf_op jit(solution)/shard_map/tail/pallas_call | solution.py:547

commit v10 on v9

--- a/solution.py
+++ b/solution.py
@@ -15,7 +15,7 @@
 AHEAD = (1, 0)
 COLUMN_FIRST = (2, 3)
 CHIPS_ALONG = (3, 1, 2, 0)
-CHIP_ORDER = tuple((other, dy) for other in (0, 1) for dy in (0, 1, -1, 2))
+CHIP_ORDER = tuple((other, dy) for other in (0, 1) for dy in (-1, 1, 0, 2))
 
 
 def turn(recv, i, put):

time: 25.7 us -> 26.7 us (1.039)
  the two profiles are of different devices: /device:TPU:97 before, /device:TPU:99 now
where the time goes in v10:
time: 26.7 us; the launch traced here: 26.6 us
  Pallas kernels  26.6 us (100%)
    pallas_call x1, Pallas kernels, run_local(): pl.pallas_call(functools.partial(conv_kernel, n_rows, n_cols), out_shape=...  24.9 us
    pallas_call x1, Pallas kernels, run_local(): pl.pallas_call(tail_kernel, out_shape=jax.ShapeDtypeStruct((tile_h, tile_...  1.71 us

profile of v10, /device:TPU:99, one launch (start us, length us, event | category | flops | bytes accessed | tf_op | source)
XLA Modules:
  0.0 26.6 jit_solution(16968419926471324003)
XLA Ops:
  0.0 24.9 %conv.1 = (f32[8,7,2,64,64]{4,3,2,1,0:T(8,128)S(1)}, bf16[5,8,2,64,128]{4,3,2,1,0:T(8,128)(2,1)S(1)}, bf16[4,256,256]{2,1,0:T(8,128)(2,1)S(1)}, f32[1,256]{1,0:T(1,128)S(1)}) custom-call(bf16[4,14,28,2,2,64]{5,4,3,2,1,0:T(2,128)(2,1)} %bitcast.8, bf16[3,3,2,64]{3,2,1,0:T(2,128)(2,1)} %w1_hbm.1, f32[1,64]{1,0:T(1,128)} %bitcast.9, ...), custom_call_target="tpu_custom_call" | custom-call | tf_op jit(solution)/shard_map/conv/pallas_call | solution.py:518
  24.9 1.7 %tail.1 = f32[7,7,2,64,64]{4,3,2,1,0:T(8,128)} custom-call(f32[8,7,2,64,64]{4,3,2,1,0:T(8,128)S(1)} %get-tuple-element.9.tile, bf16[5,8,2,64,128]{4,3,2,1,0:T(8,128)(2,1)S(1)} %get-tuple-element.10.ymat, bf16[4,256,256]{2,1,0:T(8,128)(2,1)S(1)} %get-tuple-element.11.wt2, f32[1,256]{1,0:T(1,128)S(1)} %get-tuple-element.12.bias2), custom_call_target="tpu_custom_call" | custom-call | tf_op jit(solution)/shard_map/tail/pallas_call | solution.py:547

commit v11 on v10

--- a/solution.py
+++ b/solution.py
@@ -15,7 +15,7 @@
 AHEAD = (1, 0)
 COLUMN_FIRST = (2, 3)
 CHIPS_ALONG = (3, 1, 2, 0)
-CHIP_ORDER = tuple((other, dy) for other in (0, 1) for dy in (-1, 1, 0, 2))
+CHIP_ORDER = tuple((other, dy) for other in (1, 0) for dy in (1, -1, 0, 2))
 
 
 def turn(recv, i, put):

time: 26.7 us -> 26.3 us (0.985)
  the two profiles are of different devices: /device:TPU:99 before, /device:TPU:105 now
where the time goes in v11:
time: 26.3 us; the launch traced here: 26.2 us
  Pallas kernels  26.2 us (100%)
    pallas_call x1, Pallas kernels, run_local(): pl.pallas_call(functools.partial(conv_kernel, n_rows, n_cols), out_shape=...  24.5 us
    pallas_call x1, Pallas kernels, run_local(): pl.pallas_call(tail_kernel, out_shape=jax.ShapeDtypeStruct((tile_h, tile_...  1.71 us

profile of v11, /device:TPU:105, one launch (start us, length us, event | category | flops | bytes accessed | tf_op | source)
XLA Modules:
  0.0 26.2 jit_solution(3611992586332797862)
XLA Ops:
  0.0 24.5 %conv.1 = (f32[8,7,2,64,64]{4,3,2,1,0:T(8,128)S(1)}, bf16[5,8,2,64,128]{4,3,2,1,0:T(8,128)(2,1)S(1)}, bf16[4,256,256]{2,1,0:T(8,128)(2,1)S(1)}, f32[1,256]{1,0:T(1,128)S(1)}) custom-call(bf16[4,14,28,2,2,64]{5,4,3,2,1,0:T(2,128)(2,1)} %bitcast.8, bf16[3,3,2,64]{3,2,1,0:T(2,128)(2,1)} %w1_hbm.1, f32[1,64]{1,0:T(1,128)} %bitcast.9, ...), custom_call_target="tpu_custom_call" | custom-call | tf_op jit(solution)/shard_map/conv/pallas_call | solution.py:518
  24.5 1.7 %tail.1 = f32[7,7,2,64,64]{4,3,2,1,0:T(8,128)} custom-call(f32[8,7,2,64,64]{4,3,2,1,0:T(8,128)S(1)} %get-tuple-element.9.tile, bf16[5,8,2,64,128]{4,3,2,1,0:T(8,128)(2,1)S(1)} %get-tuple-element.10.ymat, bf16[4,256,256]{2,1,0:T(8,128)(2,1)S(1)} %get-tuple-element.11.wt2, f32[1,256]{1,0:T(1,128)S(1)} %get-tuple-element.12.bias2), custom_call_target="tpu_custom_call" | custom-call | tf_op jit(solution)/shard_map/tail/pallas_call | solution.py:547

commit v12 on v7

--- a/solution.py
+++ b/solution.py
@@ -13,7 +13,7 @@
 CHUNK_ROWS = (2, 3, 2)
 TURNS, FIRSTS, SECONDS = (2, 4, 5, 6), (1, 3, 4, 5), (0, 2, 3, 3)
 AHEAD = (1, 0)
-COLUMN_FIRST = (2, 3)
+COLUMN_FIRST = (3,)
 CHIPS_ALONG = (3, 1, 2, 0)
 CHIP_ORDER = tuple((other, dy) for other in (0, 1) for dy in (1, -1, 0, 2))
 

time: 25.7 us -> 25.8 us (level); the launches traced: 25.6 us -> 25.3 us
  Pallas kernels: 25.6 us -> 25.3 us
    pallas_call x1, Pallas kernels: 23.9 us -> 23.6 us  [run_local(): pl.pallas_call(functools.partial(conv_kernel, n_rows, n_cols), out_shape=...]
where the time goes in v12:
time: 25.8 us; the launch traced here: 25.3 us
  Pallas kernels  25.3 us (98%)
    pallas_call x1, Pallas kernels, run_local(): pl.pallas_call(functools.partial(conv_kernel, n_rows, n_cols), out_shape=...  23.6 us
    pallas_call x1, Pallas kernels, run_local(): pl.pallas_call(tail_kernel, out_shape=jax.ShapeDtypeStruct((tile_h, tile_...  1.71 us

profile of v12, /device:TPU:97, one launch (start us, length us, event | category | flops | bytes accessed | tf_op | source)
XLA Modules:
  0.0 25.3 jit_solution(888917913689586419)
XLA Ops:
  0.0 23.6 %conv.1 = (f32[8,7,2,64,64]{4,3,2,1,0:T(8,128)S(1)}, bf16[5,8,2,64,128]{4,3,2,1,0:T(8,128)(2,1)S(1)}, bf16[4,256,256]{2,1,0:T(8,128)(2,1)S(1)}, f32[1,256]{1,0:T(1,128)S(1)}) custom-call(bf16[4,14,28,2,2,64]{5,4,3,2,1,0:T(2,128)(2,1)} %bitcast.8, bf16[3,3,2,64]{3,2,1,0:T(2,128)(2,1)} %w1_hbm.1, f32[1,64]{1,0:T(1,128)} %bitcast.9, ...), custom_call_target="tpu_custom_call" | custom-call | tf_op jit(solution)/shard_map/conv/pallas_call | solution.py:518
  23.6 1.7 %tail.1 = f32[7,7,2,64,64]{4,3,2,1,0:T(8,128)} custom-call(f32[8,7,2,64,64]{4,3,2,1,0:T(8,128)S(1)} %get-tuple-element.9.tile, bf16[5,8,2,64,128]{4,3,2,1,0:T(8,128)(2,1)S(1)} %get-tuple-element.10.ymat, bf16[4,256,256]{2,1,0:T(8,128)(2,1)S(1)} %get-tuple-element.11.wt2, f32[1,256]{1,0:T(1,128)S(1)} %get-tuple-element.12.bias2), custom_call_target="tpu_custom_call" | custom-call | tf_op jit(solution)/shard_map/tail/pallas_call | solution.py:547

commit v13 on v9

--- a/solution.py
+++ b/solution.py
@@ -11,7 +11,7 @@
 BF16 = jnp.bfloat16
 F32 = jnp.float32
 CHUNK_ROWS = (2, 3, 2)
-TURNS, FIRSTS, SECONDS = (2, 4, 5, 6), (1, 3, 4, 5), (0, 2, 3, 3)
+TURNS, FIRSTS, SECONDS = (2, 4, 5, 6), (1, 3, 4, 4), (0, 2, 3, 3)
 AHEAD = (1, 0)
 COLUMN_FIRST = (2, 3)
 CHIPS_ALONG = (3, 1, 2, 0)
@@ -27,24 +27,28 @@
         put(j, jnp.concatenate([top, under], axis=0).T.reshape(2, lanes // 2, 2 * chans))
 
 
-def blocks(pairs, weights, count):
+def blocks(pairs, weights, lo, count):
     acc = None
     for dw in range(4):
-        parts = [view[dw // 2 : dw // 2 + count, dw % 2] for view in pairs]
+        parts = [view[pl.ds(dw // 2 + lo, count), dw % 2] for view in pairs]
         lhs = jnp.concatenate([p.reshape(count * p.shape[1], p.shape[2]) for p in parts], axis=1)
         term = jnp.dot(lhs, weights(dw), preferred_element_type=F32)
         acc = term if acc is None else acc + term
     return acc
 
 
-def first(pairs, weights, bias, y_row, blank_a):
+def first(pairs, weights, bias, y_row, blank_a, lo, count):
+    images, lanes = y_row.shape[2:]
+    row = lax.rem(lax.broadcasted_iota(jnp.int32, (1, 2 * lanes), 1), lanes) // (lanes // 2)
+    act = jnp.maximum(blocks(pairs, weights, lo, count) + bias, 0.0)
+    act = jnp.where(row != blank_a, act, 0.0).astype(BF16)
+    for b in range(2):
+        y_row[pl.ds(lo, count), b] = act[:, b * lanes : (b + 1) * lanes].reshape(count, images, lanes)
+
+
+def blank_edges(y_row):
     count, _, images, lanes = y_row.shape
     c = lax.axis_index("cols")
-    row = lax.rem(lax.broadcasted_iota(jnp.int32, (1, 2 * lanes), 1), lanes) // (lanes // 2)
-    act = jnp.maximum(blocks(pairs, weights, count) + bias, 0.0)
-    act = jnp.where(row != blank_a, act, 0.0).astype(BF16)
-    for b in range(2):
-        y_row[:, b] = act[:, b * lanes : (b + 1) * lanes].reshape(count, images, lanes)
     blank = jnp.zeros((images, lanes), BF16)
 
     @pl.when(c == 0)
@@ -56,13 +60,13 @@
         y_row[count - 1, 1] = blank
 
 
-def second(pairs, weights, bias, out_pair):
-    _, count, _, images, chans = out_pair.shape
-    res = blocks(pairs, weights, count) + bias
+def second(pairs, weights, bias, out_pair, lo, count):
+    images, chans = out_pair.shape[3:]
+    res = blocks(pairs, weights, lo, count) + bias
     for b in range(2):
         for a in range(2):
             at = (2 * b + a) * chans
-            out_pair[a, :, b] = res[:, at : at + chans].reshape(count, images, chans)
+            out_pair[a, pl.ds(lo, count), b] = res[:, at : at + chans].reshape(count, images, chans)
 
 
 def conv_kernel(
@@ -74,13 +78,13 @@
     w2_hbm,
     b2_hbm,
     out,
+    xmat,
     ymat,
+    wt1,
     wt2,
+    bias1,
     bias2,
     recv,
-    xmat,
-    wt1,
-    bias1,
     xs,
     packed,
     w1s,
@@ -424,15 +428,16 @@
 
     def first_one(n, carry):
         i = nth(n, z_pairs)
-        fill = jnp.where(n == 0, 1 - par, 2)
-        out_of = jnp.where(n == z_pairs - 1, jnp.where(r == 0, 0, jnp.where(r == n_rows - 1, 1, 2)), 2)
-        blank_a = jnp.where(fill < 2, fill, out_of)
-        first((xmat.at[i], xmat.at[i + 1]), lambda dw: wt1[dw], bias1[...], ymat.at[i], blank_a)
+        blank_a = jnp.where(n == 0, 1 - par, 2)
+        pairs = (xmat.at[i], xmat.at[i + 1])
+        first(pairs, lambda dw: wt1[dw], bias1[...], ymat.at[i], blank_a, 0, win_j - 1)
+        blank_edges(ymat.at[i])
         return carry
 
     def second_one(n, carry):
         i = nth(n, o_pairs)
-        second((ymat.at[i], ymat.at[i + 1]), lambda dw: wt2[dw], bias2[...], out.at[pl.ds(2 * i, 2)])
+        pairs = (ymat.at[i], ymat.at[i + 1])
+        second(pairs, lambda dw: wt2[dw], bias2[...], out.at[pl.ds(2 * i, 2)], 0, tile_j)
         return carry
 
     def stage(s, carry):
@@ -473,10 +478,11 @@
             drain_own()
 
 
-def tail_kernel(tile, ymat, wt2, bias2, out_hbm, o_new, sem):
-    par = lax.rem(lax.axis_index("model"), 2)
+def tail_kernel(tile, xmat, ymat, wt1, wt2, bias1, bias2, out_hbm, y_new, o_new, sem):
+    r = lax.axis_index("model")
+    par = lax.rem(r, 2)
     rows = out_hbm.shape[0]
-    o_pairs = ymat.shape[0] - 1
+    x_pairs, z_pairs = xmat.shape[0], ymat.shape[0]
     late = (rows - 2) * par
     here = 2 * (1 - par)
 
@@ -485,12 +491,39 @@
         return carry
 
     lax.fori_loop(here, here + rows - 2, start, 0)
-    i = (o_pairs - 1) * par
-    second((ymat.at[i], ymat.at[i + 1]), lambda dw: wt2[dw], bias2[...], o_new)
-    last = pltpu.make_async_copy(o_new, out_hbm.at[pl.ds(late, 2)], sem.at[1])
-    last.start()
+    i = (x_pairs - 2) * par
+    blank_a = jnp.where(r == 0, 0, jnp.where(r == lax.axis_size("model") - 1, 1, 2))
+    half = y_new.shape[0] // 2
+
+    def first_half(h, carry):
+        first((xmat.at[i], xmat.at[i + 1]), lambda dw: wt1[dw], bias1[...], y_new, blank_a, half * h, half)
+        return carry
+
+    lax.fori_loop(0, 2, first_half, 0)
+    blank_edges(y_new)
+    depth = wt2.shape[1] // 2
+
+    def weights(dw):
+        new, old = wt2[dw, pl.ds(depth * par, depth)], wt2[dw, pl.ds(depth * (1 - par), depth)]
+        return jnp.concatenate([new, old], axis=0)
+
+    old = ymat.at[1 + (z_pairs - 3) * par]
+    count = o_new.shape[1]
+    step = count - half
+
+    def part(lo, hi, k):
+        return pltpu.make_async_copy(o_new.at[:, lo:hi], out_hbm.at[pl.ds(late, 2), lo:hi], sem.at[k])
+
+    def second_half(h, carry):
+        second((y_new, old), weights, bias2[...], o_new, step * h, half)
+        pl.when(h == 0)(lambda: part(0, step, 1).start())
+        return carry
+
+    lax.fori_loop(0, 2, second_half, 0)
+    part(step, count, 2).start()
     pltpu.make_async_copy(tile.at[0 : rows - 2], out_hbm.at[0 : rows - 2], sem.at[0]).wait()
-    last.wait()
+    part(0, step, 1).wait()
+    part(step, count, 2).wait()
 
 
 def solution(mesh):
@@ -511,8 +544,11 @@
         vmem = pl.BlockSpec(memory_space=pltpu.VMEM)
         kept = (
             pltpu.VMEM((2 * (z_pairs - 1), tile_j, 2, images, chans), F32),
+            pltpu.VMEM((x_pairs, win_j, 2, images, 2 * chans), BF16),
             pltpu.VMEM((z_pairs, win_j - 1, 2, images, 2 * chans), BF16),
             pltpu.VMEM((4, 4 * chans, 4 * chans), BF16),
+            pltpu.VMEM((4, 4 * chans, 4 * chans), BF16),
+            pltpu.VMEM((1, 4 * chans), F32),
             pltpu.VMEM((1, 4 * chans), F32),
         )
         state = pl.pallas_call(
@@ -522,9 +558,6 @@
             out_specs=[vmem] * len(kept),
             scratch_shapes=[
                 pltpu.VMEM((sources, 2 * x_pairs, win_j, own_chans, 2 * images), BF16),
-                pltpu.VMEM((x_pairs, win_j, 2, images, 2 * chans), BF16),
-                pltpu.VMEM((4, 4 * chans, 4 * chans), BF16),
-                pltpu.VMEM((1, 4 * chans), F32),
                 pltpu.VMEM((n_rows // 2, 2 * tile_h, pairs, 2, own_chans, images), BF16),
                 pltpu.VMEM((height, pairs, own_chans, 2 * images), BF16),
                 pltpu.VMEM((3, 3, own_chans, chans), BF16),
@@ -550,8 +583,9 @@
             in_specs=[vmem] * len(kept),
             out_specs=pl.BlockSpec(memory_space=pl.ANY),
             scratch_shapes=[
+                pltpu.VMEM((win_j - 1, 2, images, 2 * chans), BF16),
                 pltpu.VMEM((2, tile_j, 2, images, chans), F32),
-                pltpu.SemaphoreType.DMA((2,)),
+                pltpu.SemaphoreType.DMA((3,)),
             ],
             compiler_params=pltpu.CompilerParams(vmem_limit_bytes=8 << 20),
             name="tail",

time: 25.7 us -> 26 us (1.012)
  Pallas kernels: 25.3 us -> 25.9 us
    pallas_call x1, Pallas kernels: 1.71 us -> 2.24 us  [run_local(): pl.pallas_call(tail_kernel, out_shape=jax.ShapeDtypeStruct((tile_h, tile_...]
where the time goes in v13:
time: 26 us; the launch traced here: 25.9 us
  Pallas kernels  25.9 us (100%)
    pallas_call x1, Pallas kernels, run_local(): pl.pallas_call(functools.partial(conv_kernel, n_rows, n_cols), out_shape=...  23.6 us
    pallas_call x1, Pallas kernels, run_local(): pl.pallas_call(tail_kernel, out_shape=jax.ShapeDtypeStruct((tile_h, tile_...  2.24 us

profile of v13, /device:TPU:97, one launch (start us, length us, event | category | flops | bytes accessed | tf_op | source)
XLA Modules:
  0.0 25.9 jit_solution(4004786386832450618)
XLA Ops:
  0.0 23.6 %conv.1 = (f32[8,7,2,64,64]{4,3,2,1,0:T(8,128)S(1)}, bf16[6,9,2,64,128]{4,3,2,1,0:T(8,128)(2,1)S(1)}, bf16[5,8,2,64,128]{4,3,2,1,0:T(8,128)(2,1)S(1)}, bf16[4,25...) custom-call(bf16[4,14,28,2,2,64]{5,4,3,2,1,0:T(2,128)(2,1)} %bitcast.8,, ...), custom_call_target="tpu_custom_call" | custom-call | tf_op jit(solution)/shard_map/conv/pallas_call | solution.py:554
  23.6 2.2 %tail.1 = f32[7,7,2,64,64]{4,3,2,1,0:T(8,128)} custom-call(f32[8,7,2,64,64]{4,3,2,1,0:T(8,128)S(1)} %get-tuple-element.12.tile, bf16[6,9,2,64,128]{4,3,2,1,0:T(8,128)(2,1)S(1)} %get-tuple-element.13.xmat, bf16[5,8,2,64,128]{4,3,2,1,0:T(8,128)(2,1)S(1)} %get-tuple-element.14.ymat, bf16[4,256,256]{2,1,0:T(8,128)(2,1)S(1)} %get-tuple-element.15.wt1, ...), custom_call_target="tpu_custom_call" | custom-call | tf_op jit(solution)/shard_map/tail/pallas_call | solution.py:580

commit v14 on v9

--- a/solution.py
+++ b/solution.py
@@ -142,7 +142,7 @@
     to_rs = [lax.rem(r + k, n_rows) for k in range(n_rows)]
     for kr, kc in sorted(
         ((kr, kc) for kr in range(n_rows) for kc in range(n_cols) if kr or kc),
-        key=lambda k: (not (k[0] in (2, 3) and k[1] == 1), -(min(k[0], n_rows - k[0]) // 2 + min(k[1], n_cols - k[1]))),
+        key=lambda k: (k[1] not in (1, 2), k[0] not in (2, 3, 4, 5), k[1] == 2, k[0] < 4, -min(k[0], n_rows - k[0])),
     ):
         pl.semaphore_signal(barrier, inc=1, device_id=device(to_rs[kr], to_cs[kc]), device_id_type=MESH)
 

time: 25.7 us -> 27 us (1.051); the launches traced: 25.3 us -> 26.9 us
  Pallas kernels: 25.3 us -> 26.9 us
    pallas_call x1, Pallas kernels: 23.6 us -> 25.2 us  [run_local(): pl.pallas_call(functools.partial(conv_kernel, n_rows, n_cols), out_shape=...]
where the time goes in v14:
time: 27 us; the launch traced here: 26.9 us
  Pallas kernels  26.9 us (100%)
    pallas_call x1, Pallas kernels, run_local(): pl.pallas_call(functools.partial(conv_kernel, n_rows, n_cols), out_shape=...  25.2 us
    pallas_call x1, Pallas kernels, run_local(): pl.pallas_call(tail_kernel, out_shape=jax.ShapeDtypeStruct((tile_h, tile_...  1.71 us

profile of v14, /device:TPU:97, one launch (start us, length us, event | category | flops | bytes accessed | tf_op | source)
XLA Modules:
  0.0 26.9 jit_solution(17222691471855117891)
XLA Ops:
  0.0 25.2 %conv.1 = (f32[8,7,2,64,64]{4,3,2,1,0:T(8,128)S(1)}, bf16[5,8,2,64,128]{4,3,2,1,0:T(8,128)(2,1)S(1)}, bf16[4,256,256]{2,1,0:T(8,128)(2,1)S(1)}, f32[1,256]{1,0:T(1,128)S(1)}) custom-call(bf16[4,14,28,2,2,64]{5,4,3,2,1,0:T(2,128)(2,1)} %bitcast.8, bf16[3,3,2,64]{3,2,1,0:T(2,128)(2,1)} %w1_hbm.1, f32[1,64]{1,0:T(1,128)} %bitcast.9, ...), custom_call_target="tpu_custom_call" | custom-call | tf_op jit(solution)/shard_map/conv/pallas_call | solution.py:518
  25.2 1.7 %tail.1 = f32[7,7,2,64,64]{4,3,2,1,0:T(8,128)} custom-call(f32[8,7,2,64,64]{4,3,2,1,0:T(8,128)S(1)} %get-tuple-element.9.tile, bf16[5,8,2,64,128]{4,3,2,1,0:T(8,128)(2,1)S(1)} %get-tuple-element.10.ymat, bf16[4,256,256]{2,1,0:T(8,128)(2,1)S(1)} %get-tuple-element.11.wt2, f32[1,256]{1,0:T(1,128)S(1)} %get-tuple-element.12.bias2), custom_call_target="tpu_custom_call" | custom-call | tf_op jit(solution)/shard_map/tail/pallas_call | solution.py:547

commit v15 on v14

--- a/solution.py
+++ b/solution.py
@@ -15,7 +15,7 @@
 AHEAD = (1, 0)
 COLUMN_FIRST = (2, 3)
 CHIPS_ALONG = (3, 1, 2, 0)
-CHIP_ORDER = tuple((other, dy) for other in (0, 1) for dy in (0, 1, -1, 2))
+CHIP_ORDER = tuple((other, dy) for other in (0, 1) for dy in (1, -1, 0, 2))
 
 
 def turn(recv, i, put):

time: 27 us -> 26.9 us (level)
  the two profiles are of different devices: /device:TPU:97 before, /device:TPU:99 now
where the time goes in v15:
time: 26.9 us; the launch traced here: 26.8 us
  Pallas kernels  26.8 us (100%)
    pallas_call x1, Pallas kernels, run_local(): pl.pallas_call(functools.partial(conv_kernel, n_rows, n_cols), out_shape=...  25 us
    pallas_call x1, Pallas kernels, run_local(): pl.pallas_call(tail_kernel, out_shape=jax.ShapeDtypeStruct((tile_h, tile_...  1.71 us

profile of v15, /device:TPU:99, one launch (start us, length us, event | category | flops | bytes accessed | tf_op | source)
XLA Modules:
  0.0 26.8 jit_solution(4229296898707819860)
XLA Ops:
  0.0 25.0 %conv.1 = (f32[8,7,2,64,64]{4,3,2,1,0:T(8,128)S(1)}, bf16[5,8,2,64,128]{4,3,2,1,0:T(8,128)(2,1)S(1)}, bf16[4,256,256]{2,1,0:T(8,128)(2,1)S(1)}, f32[1,256]{1,0:T(1,128)S(1)}) custom-call(bf16[4,14,28,2,2,64]{5,4,3,2,1,0:T(2,128)(2,1)} %bitcast.8, bf16[3,3,2,64]{3,2,1,0:T(2,128)(2,1)} %w1_hbm.1, f32[1,64]{1,0:T(1,128)} %bitcast.9, ...), custom_call_target="tpu_custom_call" | custom-call | tf_op jit(solution)/shard_map/conv/pallas_call | solution.py:518
  25.1 1.7 %tail.1 = f32[7,7,2,64,64]{4,3,2,1,0:T(8,128)} custom-call(f32[8,7,2,64,64]{4,3,2,1,0:T(8,128)S(1)} %get-tuple-element.9.tile, bf16[5,8,2,64,128]{4,3,2,1,0:T(8,128)(2,1)S(1)} %get-tuple-element.10.ymat, bf16[4,256,256]{2,1,0:T(8,128)(2,1)S(1)} %get-tuple-element.11.wt2, f32[1,256]{1,0:T(1,128)S(1)} %get-tuple-element.12.bias2), custom_call_target="tpu_custom_call" | custom-call | tf_op jit(solution)/shard_map/tail/pallas_call | solution.py:547

commit v16 on v14

--- a/solution.py
+++ b/solution.py
@@ -13,7 +13,7 @@
 CHUNK_ROWS = (2, 3, 2)
 TURNS, FIRSTS, SECONDS = (2, 4, 5, 6), (1, 3, 4, 5), (0, 2, 3, 3)
 AHEAD = (1, 0)
-COLUMN_FIRST = (2, 3)
+COLUMN_FIRST = (3,)
 CHIPS_ALONG = (3, 1, 2, 0)
 CHIP_ORDER = tuple((other, dy) for other in (0, 1) for dy in (0, 1, -1, 2))
 

time: 27 us -> 27.9 us (1.033)
  Pallas kernels: 26.9 us -> 27.8 us
    pallas_call x1, Pallas kernels: 25.2 us -> 26.1 us  [run_local(): pl.pallas_call(functools.partial(conv_kernel, n_rows, n_cols), out_shape=...]
where the time goes in v16:
time: 27.9 us; the launch traced here: 27.8 us
  Pallas kernels  27.8 us (100%)
    pallas_call x1, Pallas kernels, run_local(): pl.pallas_call(functools.partial(conv_kernel, n_rows, n_cols), out_shape=...  26.1 us
    pallas_call x1, Pallas kernels, run_local(): pl.pallas_call(tail_kernel, out_shape=jax.ShapeDtypeStruct((tile_h, tile_...  1.71 us

profile of v16, /device:TPU:97, one launch (start us, length us, event | category | flops | bytes accessed | tf_op | source)
XLA Modules:
  0.0 27.8 jit_solution(13883610581255194593)
XLA Ops:
  0.0 26.1 %conv.1 = (f32[8,7,2,64,64]{4,3,2,1,0:T(8,128)S(1)}, bf16[5,8,2,64,128]{4,3,2,1,0:T(8,128)(2,1)S(1)}, bf16[4,256,256]{2,1,0:T(8,128)(2,1)S(1)}, f32[1,256]{1,0:T(1,128)S(1)}) custom-call(bf16[4,14,28,2,2,64]{5,4,3,2,1,0:T(2,128)(2,1)} %bitcast.8, bf16[3,3,2,64]{3,2,1,0:T(2,128)(2,1)} %w1_hbm.1, f32[1,64]{1,0:T(1,128)} %bitcast.9, ...), custom_call_target="tpu_custom_call" | custom-call | tf_op jit(solution)/shard_map/conv/pallas_call | solution.py:518
  26.1 1.7 %tail.1 = f32[7,7,2,64,64]{4,3,2,1,0:T(8,128)} custom-call(f32[8,7,2,64,64]{4,3,2,1,0:T(8,128)S(1)} %get-tuple-element.9.tile, bf16[5,8,2,64,128]{4,3,2,1,0:T(8,128)(2,1)S(1)} %get-tuple-element.10.ymat, bf16[4,256,256]{2,1,0:T(8,128)(2,1)S(1)} %get-tuple-element.11.wt2, f32[1,256]{1,0:T(1,128)S(1)} %get-tuple-element.12.bias2), custom_call_target="tpu_custom_call" | custom-call | tf_op jit(solution)/shard_map/tail/pallas_call | solution.py:547

commit v17 on v16

--- a/solution.py
+++ b/solution.py
@@ -15,7 +15,7 @@
 AHEAD = (1, 0)
 COLUMN_FIRST = (3,)
 CHIPS_ALONG = (3, 1, 2, 0)
-CHIP_ORDER = tuple((other, dy) for other in (0, 1) for dy in (0, 1, -1, 2))
+CHIP_ORDER = tuple((other, dy) for other in (0, 1) for dy in (1, -1, 0, 2))
 
 
 def turn(recv, i, put):

time: 27.9 us -> 26.5 us (0.950); the launches traced: 27.8 us -> 26 us
  Pallas kernels: 27.8 us -> 26 us
    pallas_call x1, Pallas kernels: 26.1 us -> 24.3 us  [run_local(): pl.pallas_call(functools.partial(conv_kernel, n_rows, n_cols), out_shape=...]
where the time goes in v17:
time: 26.5 us; the launch traced here: 26 us
  Pallas kernels  26 us (98%)
    pallas_call x1, Pallas kernels, run_local(): pl.pallas_call(functools.partial(conv_kernel, n_rows, n_cols), out_shape=...  24.3 us
    pallas_call x1, Pallas kernels, run_local(): pl.pallas_call(tail_kernel, out_shape=jax.ShapeDtypeStruct((tile_h, tile_...  1.71 us

profile of v17, /device:TPU:97, one launch (start us, length us, event | category | flops | bytes accessed | tf_op | source)
XLA Modules:
  0.0 26.0 jit_solution(15740559975992477308)
XLA Ops:
  0.0 24.3 %conv.1 = (f32[8,7,2,64,64]{4,3,2,1,0:T(8,128)S(1)}, bf16[5,8,2,64,128]{4,3,2,1,0:T(8,128)(2,1)S(1)}, bf16[4,256,256]{2,1,0:T(8,128)(2,1)S(1)}, f32[1,256]{1,0:T(1,128)S(1)}) custom-call(bf16[4,14,28,2,2,64]{5,4,3,2,1,0:T(2,128)(2,1)} %bitcast.8, bf16[3,3,2,64]{3,2,1,0:T(2,128)(2,1)} %w1_hbm.1, f32[1,64]{1,0:T(1,128)} %bitcast.9, ...), custom_call_target="tpu_custom_call" | custom-call | tf_op jit(solution)/shard_map/conv/pallas_call | solution.py:518
  24.3 1.7 %tail.1 = f32[7,7,2,64,64]{4,3,2,1,0:T(8,128)} custom-call(f32[8,7,2,64,64]{4,3,2,1,0:T(8,128)S(1)} %get-tuple-element.9.tile, bf16[5,8,2,64,128]{4,3,2,1,0:T(8,128)(2,1)S(1)} %get-tuple-element.10.ymat, bf16[4,256,256]{2,1,0:T(8,128)(2,1)S(1)} %get-tuple-element.11.wt2, f32[1,256]{1,0:T(1,128)S(1)} %get-tuple-element.12.bias2), custom_call_target="tpu_custom_call" | custom-call | tf_op jit(solution)/shard_map/tail/pallas_call | solution.py:547

commit v18 on v15

--- a/solution.py
+++ b/solution.py
@@ -14,7 +14,7 @@
 TURNS, FIRSTS, SECONDS = (2, 4, 5, 6), (1, 3, 4, 5), (0, 2, 3, 3)
 AHEAD = (1, 0)
 COLUMN_FIRST = (2, 3)
-CHIPS_ALONG = (3, 1, 2, 0)
+CHIPS_ALONG = (1, 3, 2, 0)
 CHIP_ORDER = tuple((other, dy) for other in (0, 1) for dy in (1, -1, 0, 2))
 
 

time: 26.9 us -> 27.3 us (1.015)
  Pallas kernels: 26.8 us -> 27.2 us
    pallas_call x1, Pallas kernels: 25 us -> 25.5 us  [run_local(): pl.pallas_call(functools.partial(conv_kernel, n_rows, n_cols), out_shape=...]
where the time goes in v18:
time: 27.3 us; the launch traced here: 27.2 us
  Pallas kernels  27.2 us (100%)
    pallas_call x1, Pallas kernels, run_local(): pl.pallas_call(functools.partial(conv_kernel, n_rows, n_cols), out_shape=...  25.5 us
    pallas_call x1, Pallas kernels, run_local(): pl.pallas_call(tail_kernel, out_shape=jax.ShapeDtypeStruct((tile_h, tile_...  1.71 us

profile of v18, /device:TPU:99, one launch (start us, length us, event | category | flops | bytes accessed | tf_op | source)
XLA Modules:
  0.0 27.2 jit_solution(17304723244121285892)
XLA Ops:
  0.0 25.5 %conv.1 = (f32[8,7,2,64,64]{4,3,2,1,0:T(8,128)S(1)}, bf16[5,8,2,64,128]{4,3,2,1,0:T(8,128)(2,1)S(1)}, bf16[4,256,256]{2,1,0:T(8,128)(2,1)S(1)}, f32[1,256]{1,0:T(1,128)S(1)}) custom-call(bf16[4,14,28,2,2,64]{5,4,3,2,1,0:T(2,128)(2,1)} %bitcast.8, bf16[3,3,2,64]{3,2,1,0:T(2,128)(2,1)} %w1_hbm.1, f32[1,64]{1,0:T(1,128)} %bitcast.9, ...), custom_call_target="tpu_custom_call" | custom-call | tf_op jit(solution)/shard_map/conv/pallas_call | solution.py:518
  25.5 1.7 %tail.1 = f32[7,7,2,64,64]{4,3,2,1,0:T(8,128)} custom-call(f32[8,7,2,64,64]{4,3,2,1,0:T(8,128)S(1)} %get-tuple-element.9.tile, bf16[5,8,2,64,128]{4,3,2,1,0:T(8,128)(2,1)S(1)} %get-tuple-element.10.ymat, bf16[4,256,256]{2,1,0:T(8,128)(2,1)S(1)} %get-tuple-element.11.wt2, f32[1,256]{1,0:T(1,128)S(1)} %get-tuple-element.12.bias2), custom_call_target="tpu_custom_call" | custom-call | tf_op jit(solution)/shard_map/tail/pallas_call | solution.py:547

commit v19 on v18

--- a/solution.py
+++ b/solution.py
@@ -15,7 +15,7 @@
 AHEAD = (1, 0)
 COLUMN_FIRST = (2, 3)
 CHIPS_ALONG = (1, 3, 2, 0)
-CHIP_ORDER = tuple((other, dy) for other in (0, 1) for dy in (1, -1, 0, 2))
+CHIP_ORDER = tuple((other, dy) for other in (0, 1) for dy in (0, 1, -1, 2))
 
 
 def turn(recv, i, put):

time: 27.3 us -> 26.2 us (0.960)
  the two profiles are of different devices: /device:TPU:99 before, /device:TPU:97 now
where the time goes in v19:
time: 26.2 us; the launch traced here: 25.9 us
  Pallas kernels  25.9 us (99%)
    pallas_call x1, Pallas kernels, run_local(): pl.pallas_call(functools.partial(conv_kernel, n_rows, n_cols), out_shape=...  24.2 us
    pallas_call x1, Pallas kernels, run_local(): pl.pallas_call(tail_kernel, out_shape=jax.ShapeDtypeStruct((tile_h, tile_...  1.71 us

profile of v19, /device:TPU:97, one launch (start us, length us, event | category | flops | bytes accessed | tf_op | source)
XLA Modules:
  0.0 25.9 jit_solution(14895110778858984555)
XLA Ops:
  0.0 24.2 %conv.1 = (f32[8,7,2,64,64]{4,3,2,1,0:T(8,128)S(1)}, bf16[5,8,2,64,128]{4,3,2,1,0:T(8,128)(2,1)S(1)}, bf16[4,256,256]{2,1,0:T(8,128)(2,1)S(1)}, f32[1,256]{1,0:T(1,128)S(1)}) custom-call(bf16[4,14,28,2,2,64]{5,4,3,2,1,0:T(2,128)(2,1)} %bitcast.8, bf16[3,3,2,64]{3,2,1,0:T(2,128)(2,1)} %w1_hbm.1, f32[1,64]{1,0:T(1,128)} %bitcast.9, ...), custom_call_target="tpu_custom_call" | custom-call | tf_op jit(solution)/shard_map/conv/pallas_call | solution.py:518
  24.2 1.7 %tail.1 = f32[7,7,2,64,64]{4,3,2,1,0:T(8,128)} custom-call(f32[8,7,2,64,64]{4,3,2,1,0:T(8,128)S(1)} %get-tuple-element.9.tile, bf16[5,8,2,64,128]{4,3,2,1,0:T(8,128)(2,1)S(1)} %get-tuple-element.10.ymat, bf16[4,256,256]{2,1,0:T(8,128)(2,1)S(1)} %get-tuple-element.11.wt2, f32[1,256]{1,0:T(1,128)S(1)} %get-tuple-element.12.bias2), custom_call_target="tpu_custom_call" | custom-call | tf_op jit(solution)/shard_map/tail/pallas_call | solution.py:547

commit v20 on v15

--- a/solution.py
+++ b/solution.py
@@ -284,7 +284,7 @@
     def pack_and_send(t, carry):
         pl.when(t < chips - 1)(lambda: pack_rows(turn_to(t + 1)[0], *groups[0][0]))
         send_chip(0, t, False)
-        pl.when(t == 0)(send_weights)
+        pl.when(t == chips - 1)(send_weights)
         return carry
 
     lax.fori_loop(0, chips, pack_and_send, 0)

time: 26.9 us -> 26.1 us (0.970)
  the two profiles are of different devices: /device:TPU:99 before, /device:TPU:97 now
where the time goes in v20:
time: 26.1 us; the launch traced here: 26 us
  Pallas kernels  26 us (100%)
    pallas_call x1, Pallas kernels, run_local(): pl.pallas_call(functools.partial(conv_kernel, n_rows, n_cols), out_shape=...  24.2 us
    pallas_call x1, Pallas kernels, run_local(): pl.pallas_call(tail_kernel, out_shape=jax.ShapeDtypeStruct((tile_h, tile_...  1.71 us

profile of v20, /device:TPU:97, one launch (start us, length us, event | category | flops | bytes accessed | tf_op | source)
XLA Modules:
  0.0 26.0 jit_solution(8095949409581166939)
XLA Ops:
  0.0 24.2 %conv.1 = (f32[8,7,2,64,64]{4,3,2,1,0:T(8,128)S(1)}, bf16[5,8,2,64,128]{4,3,2,1,0:T(8,128)(2,1)S(1)}, bf16[4,256,256]{2,1,0:T(8,128)(2,1)S(1)}, f32[1,256]{1,0:T(1,128)S(1)}) custom-call(bf16[4,14,28,2,2,64]{5,4,3,2,1,0:T(2,128)(2,1)} %bitcast.8, bf16[3,3,2,64]{3,2,1,0:T(2,128)(2,1)} %w1_hbm.1, f32[1,64]{1,0:T(1,128)} %bitcast.9, ...), custom_call_target="tpu_custom_call" | custom-call | tf_op jit(solution)/shard_map/conv/pallas_call | solution.py:518
  24.3 1.7 %tail.1 = f32[7,7,2,64,64]{4,3,2,1,0:T(8,128)} custom-call(f32[8,7,2,64,64]{4,3,2,1,0:T(8,128)S(1)} %get-tuple-element.9.tile, bf16[5,8,2,64,128]{4,3,2,1,0:T(8,128)(2,1)S(1)} %get-tuple-element.10.ymat, bf16[4,256,256]{2,1,0:T(8,128)(2,1)S(1)} %get-tuple-element.11.wt2, f32[1,256]{1,0:T(1,128)S(1)} %get-tuple-element.12.bias2), custom_call_target="tpu_custom_call" | custom-call | tf_op jit(solution)/shard_map/tail/pallas_call | solution.py:547

commit v21 on v9

--- a/solution.py
+++ b/solution.py
@@ -12,8 +12,7 @@
 F32 = jnp.float32
 CHUNK_ROWS = (2, 3, 2)
 TURNS, FIRSTS, SECONDS = (2, 4, 5, 6), (1, 3, 4, 5), (0, 2, 3, 3)
-AHEAD = (1, 0)
-COLUMN_FIRST = (2, 3)
+EARLY_FROM = 1
 CHIPS_ALONG = (3, 1, 2, 0)
 CHIP_ORDER = tuple((other, dy) for other in (0, 1) for dy in (0, 1, -1, 2))
 
@@ -205,7 +204,6 @@
         pl.when(there & jnp.logical_not(edge))(lambda: copy(win_j, tile_j * to_c - 1, 0))
 
     chips = n_rows // 2
-    ahead_r, ahead_c = AHEAD
 
     def step(t, table):
         value = jnp.int32(table[-1])
@@ -217,7 +215,7 @@
         dx = step(t, CHIPS_ALONG)
         return lax.rem(r // 2 + dx, chips), dx
 
-    def send_chip(chunk, t, rest, where=None):
+    def send_chip(chunk, t, where=None):
         x, dx = turn_to(t)
         way = 1 - 2 * lax.rem(par + t, 2)
         for other, dy in CHIP_ORDER:
@@ -226,32 +224,20 @@
             there = True
             if not other and dy == 0:
                 there = dx > 0
-            if rest:
-                there = there & jnp.logical_not((to_r == ahead_r) & (to_c == ahead_c))
             if where is not None:
                 there = there & where(to_c)
             send_tile(chunk, to_r, to_c, there)
 
-    def send_ahead(chunk):
-        send_tile(chunk, jnp.int32(ahead_r), jnp.int32(ahead_c), (r != ahead_r) | (c != ahead_c))
-
     def send_chunk(chunk):
-
-        def first_column(t, carry):
-            x, _ = turn_to(t)
-            for other in range(2):
-                to_r = 2 * x + (1 - par if other else par)
-                there = ((to_r != r) | (c != 0)) & (to_r != ahead_r)
-                send_tile(chunk, to_r, jnp.int32(0), there)
-            return carry
-
-        where = None
-        if chunk in COLUMN_FIRST:
-            lax.fori_loop(0, chips, first_column, 0)
-            where = lambda to_c: to_c > 0
+        early = EARLY_FROM <= chunk
 
         def body(t, carry):
-            send_chip(chunk, t, True, where)
+            send_chip(chunk, t, (lambda to_c: to_c > 0) if early and chunk > EARLY_FROM else None)
+            if early and chunk + 1 < len(chunks):
+                x, dx = turn_to(t)
+                for other in range(2):
+                    to_r = 2 * x + (1 - par if other else par)
+                    send_tile(chunk + 1, to_r, jnp.int32(0), (to_r != r) | (c != 0))
             return carry
 
         lax.fori_loop(0, chips, body, 0)
@@ -283,20 +269,18 @@
 
     def pack_and_send(t, carry):
         pl.when(t < chips - 1)(lambda: pack_rows(turn_to(t + 1)[0], *groups[0][0]))
-        send_chip(0, t, False)
+        send_chip(0, t)
         pl.when(t == 0)(send_weights)
         return carry
 
     lax.fori_loop(0, chips, pack_and_send, 0)
 
-    pack(1)
-    send_ahead(1)
-    send_chunk(1)
-    pack(2)
-    send_ahead(2)
-    send_ahead(3)
-    send_chunk(2)
-    send_chunk(3)
+    for g in range(1, EARLY_FROM + 1):
+        pack(g)
+    for chunk in range(1, len(chunks)):
+        if chunk >= EARLY_FROM and chunk + 1 < len(groups):
+            pack(chunk + 1)
+        send_chunk(chunk)
 
     def wait_bytes(ref, sem):
         pltpu.make_async_copy(ref, ref, sem).wait()

time: 25.7 us -> 27.1 us (1.054); the launches traced: 25.3 us -> 27 us
  Pallas kernels: 25.3 us -> 27 us
    pallas_call x1, Pallas kernels: 23.6 us -> 25.3 us  [run_local(): pl.pallas_call(functools.partial(conv_kernel, n_rows, n_cols), out_shape=...]
where the time goes in v21:
time: 27.1 us; the launch traced here: 27 us
  Pallas kernels  27 us (100%)
    pallas_call x1, Pallas kernels, run_local(): pl.pallas_call(functools.partial(conv_kernel, n_rows, n_cols), out_shape=...  25.3 us
    pallas_call x1, Pallas kernels, run_local(): pl.pallas_call(tail_kernel, out_shape=jax.ShapeDtypeStruct((tile_h, tile_...  1.71 us

profile of v21, /device:TPU:97, one launch (start us, length us, event | category | flops | bytes accessed | tf_op | source)
XLA Modules:
  0.0 27.0 jit_solution(12372677361954123358)
XLA Ops:
  0.0 25.3 %conv.1 = (f32[8,7,2,64,64]{4,3,2,1,0:T(8,128)S(1)}, bf16[5,8,2,64,128]{4,3,2,1,0:T(8,128)(2,1)S(1)}, bf16[4,256,256]{2,1,0:T(8,128)(2,1)S(1)}, f32[1,256]{1,0:T(1,128)S(1)}) custom-call(bf16[4,14,28,2,2,64]{5,4,3,2,1,0:T(2,128)(2,1)} %bitcast.8, bf16[3,3,2,64]{3,2,1,0:T(2,128)(2,1)} %w1_hbm.1, f32[1,64]{1,0:T(1,128)} %bitcast.9, ...), custom_call_target="tpu_custom_call" | custom-call | tf_op jit(solution)/shard_map/conv/pallas_call | solution.py:502
  25.3 1.7 %tail.1 = f32[7,7,2,64,64]{4,3,2,1,0:T(8,128)} custom-call(f32[8,7,2,64,64]{4,3,2,1,0:T(8,128)S(1)} %get-tuple-element.9.tile, bf16[5,8,2,64,128]{4,3,2,1,0:T(8,128)(2,1)S(1)} %get-tuple-element.10.ymat, bf16[4,256,256]{2,1,0:T(8,128)(2,1)S(1)} %get-tuple-element.11.wt2, f32[1,256]{1,0:T(1,128)S(1)} %get-tuple-element.12.bias2), custom_call_target="tpu_custom_call" | custom-call | tf_op jit(solution)/shard_map/tail/pallas_call | solution.py:531

commit v22 on v21

--- a/solution.py
+++ b/solution.py
@@ -12,7 +12,7 @@
 F32 = jnp.float32
 CHUNK_ROWS = (2, 3, 2)
 TURNS, FIRSTS, SECONDS = (2, 4, 5, 6), (1, 3, 4, 5), (0, 2, 3, 3)
-EARLY_FROM = 1
+EARLY_FROM = 2
 CHIPS_ALONG = (3, 1, 2, 0)
 CHIP_ORDER = tuple((other, dy) for other in (0, 1) for dy in (0, 1, -1, 2))
 

time: 27.1 us -> 27.6 us (1.018)
  Pallas kernels: 27 us -> 27.5 us
    pallas_call x1, Pallas kernels: 25.3 us -> 25.8 us  [run_local(): pl.pallas_call(functools.partial(conv_kernel, n_rows, n_cols), out_shape=...]
where the time goes in v22:
time: 27.6 us; the launch traced here: 27.5 us
  Pallas kernels  27.5 us (100%)
    pallas_call x1, Pallas kernels, run_local(): pl.pallas_call(functools.partial(conv_kernel, n_rows, n_cols), out_shape=...  25.8 us
    pallas_call x1, Pallas kernels, run_local(): pl.pallas_call(tail_kernel, out_shape=jax.ShapeDtypeStruct((tile_h, tile_...  1.71 us

profile of v22, /device:TPU:97, one launch (start us, length us, event | category | flops | bytes accessed | tf_op | source)
XLA Modules:
  0.0 27.5 jit_solution(14337031896112225495)
XLA Ops:
  0.0 25.8 %conv.1 = (f32[8,7,2,64,64]{4,3,2,1,0:T(8,128)S(1)}, bf16[5,8,2,64,128]{4,3,2,1,0:T(8,128)(2,1)S(1)}, bf16[4,256,256]{2,1,0:T(8,128)(2,1)S(1)}, f32[1,256]{1,0:T(1,128)S(1)}) custom-call(bf16[4,14,28,2,2,64]{5,4,3,2,1,0:T(2,128)(2,1)} %bitcast.8, bf16[3,3,2,64]{3,2,1,0:T(2,128)(2,1)} %w1_hbm.1, f32[1,64]{1,0:T(1,128)} %bitcast.9, ...), custom_call_target="tpu_custom_call" | custom-call | tf_op jit(solution)/shard_map/conv/pallas_call | solution.py:502
  25.8 1.7 %tail.1 = f32[7,7,2,64,64]{4,3,2,1,0:T(8,128)} custom-call(f32[8,7,2,64,64]{4,3,2,1,0:T(8,128)S(1)} %get-tuple-element.9.tile, bf16[5,8,2,64,128]{4,3,2,1,0:T(8,128)(2,1)S(1)} %get-tuple-element.10.ymat, bf16[4,256,256]{2,1,0:T(8,128)(2,1)S(1)} %get-tuple-element.11.wt2, f32[1,256]{1,0:T(1,128)S(1)} %get-tuple-element.12.bias2), custom_call_target="tpu_custom_call" | custom-call | tf_op jit(solution)/shard_map/tail/pallas_call | solution.py:531

commit v23 on v21

--- a/solution.py
+++ b/solution.py
@@ -13,6 +13,7 @@
 CHUNK_ROWS = (2, 3, 2)
 TURNS, FIRSTS, SECONDS = (2, 4, 5, 6), (1, 3, 4, 5), (0, 2, 3, 3)
 EARLY_FROM = 1
+AHEAD = (1, 0)
 CHIPS_ALONG = (3, 1, 2, 0)
 CHIP_ORDER = tuple((other, dy) for other in (0, 1) for dy in (0, 1, -1, 2))
 
@@ -145,6 +146,9 @@
     ):
         pl.semaphore_signal(barrier, inc=1, device_id=device(to_rs[kr], to_cs[kc]), device_id_type=MESH)
 
+    ahead_r, ahead_c = AHEAD
+    is_ahead = (r == ahead_r) & (c == ahead_c)
+
     def pack_rows(x, lo, hi):
         rows = hi - lo
         left, right = (xs[x, lo:hi, :, p].reshape(rows * pairs * 2, images) for p in range(2))
@@ -152,12 +156,16 @@
         packed[pl.ds(chip_h * x + lo, rows)] = both.reshape(rows, pairs, 2, 2 * images)
 
     def pack(g):
-        for copy in loads[g]:
-            copy.wait()
+        for n, copy in enumerate(loads[g]):
+            if (g, n) != (1, ahead_r % 2):
+                copy.wait()
 
         def body(x, carry):
-            for lo, hi in groups[g]:
-                pack_rows(x, lo, hi)
+            for n, (lo, hi) in enumerate(groups[g]):
+                if (g, n) == (1, ahead_r % 2):
+                    pl.when(x != ahead_r // 2)(lambda lo=lo, hi=hi: pack_rows(x, lo, hi))
+                else:
+                    pack_rows(x, lo, hi)
             return carry
 
         lax.fori_loop(0, n_rows // 2, body, 0)
@@ -225,19 +233,28 @@
             if not other and dy == 0:
                 there = dx > 0
             if where is not None:
-                there = there & where(to_c)
+                there = there & where(to_r, to_c)
             send_tile(chunk, to_r, to_c, there)
 
     def send_chunk(chunk):
         early = EARLY_FROM <= chunk
 
         def body(t, carry):
-            send_chip(chunk, t, (lambda to_c: to_c > 0) if early and chunk > EARLY_FROM else None)
+            if chunk > EARLY_FROM:
+                send_chip(chunk, t, lambda to_r, to_c: to_c > 0)
+            else:
+                send_chip(chunk, t, lambda to_r, to_c: (to_r != ahead_r) | (to_c != ahead_c))
             if early and chunk + 1 < len(chunks):
                 x, dx = turn_to(t)
                 for other in range(2):
                     to_r = 2 * x + (1 - par if other else par)
-                    send_tile(chunk + 1, to_r, jnp.int32(0), (to_r != r) | (c != 0))
+                    there = (to_r != r) | (c != 0)
+                    if chunk > EARLY_FROM:
+                        there = there & (to_r != ahead_r)
+                    send_tile(chunk + 1, to_r, jnp.int32(0), there)
+                if chunk == EARLY_FROM:
+                    there = (x == ahead_r // 2) & jnp.logical_not(is_ahead)
+                    send_tile(len(chunks) - 1, jnp.int32(ahead_r), jnp.int32(ahead_c), there)
             return carry
 
         lax.fori_loop(0, chips, body, 0)
@@ -269,7 +286,15 @@
 
     def pack_and_send(t, carry):
         pl.when(t < chips - 1)(lambda: pack_rows(turn_to(t + 1)[0], *groups[0][0]))
+        there = turn_to(t)[0] == ahead_r // 2
+
+        @pl.when(there)
+        def _():
+            loads[1][ahead_r % 2].wait()
+            pack_rows(ahead_r // 2, *groups[1][ahead_r % 2])
+
         send_chip(0, t)
+        send_tile(1, jnp.int32(ahead_r), jnp.int32(ahead_c), there & jnp.logical_not(is_ahead))
         pl.when(t == 0)(send_weights)
         return carry
 

time: 27.1 us -> 25.7 us (0.948); the launches traced: 27 us -> 25.4 us
  Pallas kernels: 27 us -> 25.3 us
    pallas_call x1, Pallas kernels: 25.3 us -> 23.6 us  [run_local(): pl.pallas_call(functools.partial(conv_kernel, n_rows, n_cols), out_shape=...]
where the time goes in v23:
time: 25.7 us; the launch traced here: 25.4 us
  Pallas kernels  25.3 us (98%)
    pallas_call x1, Pallas kernels, run_local(): pl.pallas_call(functools.partial(conv_kernel, n_rows, n_cols), out_shape=...  23.6 us
    pallas_call x1, Pallas kernels, run_local(): pl.pallas_call(tail_kernel, out_shape=jax.ShapeDtypeStruct((tile_h, tile_...  1.71 us

profile of v23, /device:TPU:97, one launch (start us, length us, event | category | flops | bytes accessed | tf_op | source)
XLA Modules:
  0.0 25.4 jit_solution(4791523655338640120)
XLA Ops:
  0.0 23.6 %conv.1 = (f32[8,7,2,64,64]{4,3,2,1,0:T(8,128)S(1)}, bf16[5,8,2,64,128]{4,3,2,1,0:T(8,128)(2,1)S(1)}, bf16[4,256,256]{2,1,0:T(8,128)(2,1)S(1)}, f32[1,256]{1,0:T(1,128)S(1)}) custom-call(bf16[4,14,28,2,2,64]{5,4,3,2,1,0:T(2,128)(2,1)} %bitcast.8, bf16[3,3,2,64]{3,2,1,0:T(2,128)(2,1)} %w1_hbm.1, f32[1,64]{1,0:T(1,128)} %bitcast.9, ...), custom_call_target="tpu_custom_call" | custom-call | tf_op jit(solution)/shard_map/conv/pallas_call | solution.py:527
  23.6 1.7 %tail.1 = f32[7,7,2,64,64]{4,3,2,1,0:T(8,128)} custom-call(f32[8,7,2,64,64]{4,3,2,1,0:T(8,128)S(1)} %get-tuple-element.9.tile, bf16[5,8,2,64,128]{4,3,2,1,0:T(8,128)(2,1)S(1)} %get-tuple-element.10.ymat, bf16[4,256,256]{2,1,0:T(8,128)(2,1)S(1)} %get-tuple-element.11.wt2, f32[1,256]{1,0:T(1,128)S(1)} %get-tuple-element.12.bias2), custom_call_target="tpu_custom_call" | custom-call | tf_op jit(solution)/shard_map/tail/pallas_call | solution.py:556

commit v24 on v23

--- a/solution.py
+++ b/solution.py
@@ -142,7 +142,7 @@
     to_rs = [lax.rem(r + k, n_rows) for k in range(n_rows)]
     for kr, kc in sorted(
         ((kr, kc) for kr in range(n_rows) for kc in range(n_cols) if kr or kc),
-        key=lambda k: (not (k[0] in (2, 3) and k[1] == 1), -(min(k[0], n_rows - k[0]) // 2 + min(k[1], n_cols - k[1]))),
+        key=lambda k: (k[1] not in (1, 2), k[0] not in (2, 3, 4, 5), k[1] == 2, k[0] < 4, -min(k[0], n_rows - k[0])),
     ):
         pl.semaphore_signal(barrier, inc=1, device_id=device(to_rs[kr], to_cs[kc]), device_id_type=MESH)
 

time: 25.7 us -> 25.5 us (level)
  no operation moved by 1% of the time
where the time goes in v24:
time: 25.5 us; the launch traced here: 25.3 us
  Pallas kernels  25.3 us (99%)
    pallas_call x1, Pallas kernels, run_local(): pl.pallas_call(functools.partial(conv_kernel, n_rows, n_cols), out_shape=...  23.6 us
    pallas_call x1, Pallas kernels, run_local(): pl.pallas_call(tail_kernel, out_shape=jax.ShapeDtypeStruct((tile_h, tile_...  1.71 us

profile of v24, /device:TPU:97, one launch (start us, length us, event | category | flops | bytes accessed | tf_op | source)
XLA Modules:
  0.0 25.3 jit_solution(12435128033414729430)
XLA Ops:
  0.0 23.6 %conv.1 = (f32[8,7,2,64,64]{4,3,2,1,0:T(8,128)S(1)}, bf16[5,8,2,64,128]{4,3,2,1,0:T(8,128)(2,1)S(1)}, bf16[4,256,256]{2,1,0:T(8,128)(2,1)S(1)}, f32[1,256]{1,0:T(1,128)S(1)}) custom-call(bf16[4,14,28,2,2,64]{5,4,3,2,1,0:T(2,128)(2,1)} %bitcast.8, bf16[3,3,2,64]{3,2,1,0:T(2,128)(2,1)} %w1_hbm.1, f32[1,64]{1,0:T(1,128)} %bitcast.9, ...), custom_call_target="tpu_custom_call" | custom-call | tf_op jit(solution)/shard_map/conv/pallas_call | solution.py:527
  23.6 1.7 %tail.1 = f32[7,7,2,64,64]{4,3,2,1,0:T(8,128)} custom-call(f32[8,7,2,64,64]{4,3,2,1,0:T(8,128)S(1)} %get-tuple-element.9.tile, bf16[5,8,2,64,128]{4,3,2,1,0:T(8,128)(2,1)S(1)} %get-tuple-element.10.ymat, bf16[4,256,256]{2,1,0:T(8,128)(2,1)S(1)} %get-tuple-element.11.wt2, f32[1,256]{1,0:T(1,128)S(1)} %get-tuple-element.12.bias2), custom_call_target="tpu_custom_call" | custom-call | tf_op jit(solution)/shard_map/tail/pallas_call | solution.py:556

commit v25 on v23

--- a/solution.py
+++ b/solution.py
@@ -15,7 +15,7 @@
 EARLY_FROM = 1
 AHEAD = (1, 0)
 CHIPS_ALONG = (3, 1, 2, 0)
-CHIP_ORDER = tuple((other, dy) for other in (0, 1) for dy in (0, 1, -1, 2))
+CHIP_ORDER = tuple((other, dy) for other in (0, 1) for dy in (1, -1, 0, 2))
 
 
 def turn(recv, i, put):

time: 25.7 us -> 27.2 us (1.058)
  the two profiles are of different devices: /device:TPU:97 before, /device:TPU:101 now
where the time goes in v25:
time: 27.2 us; the launch traced here: 27.1 us
  Pallas kernels  27.1 us (100%)
    pallas_call x1, Pallas kernels, run_local(): pl.pallas_call(functools.partial(conv_kernel, n_rows, n_cols), out_shape=...  25.4 us
    pallas_call x1, Pallas kernels, run_local(): pl.pallas_call(tail_kernel, out_shape=jax.ShapeDtypeStruct((tile_h, tile_...  1.71 us

profile of v25, /device:TPU:101, one launch (start us, length us, event | category | flops | bytes accessed | tf_op | source)
XLA Modules:
  0.0 27.1 jit_solution(13999643650516403613)
XLA Ops:
  0.0 25.4 %conv.1 = (f32[8,7,2,64,64]{4,3,2,1,0:T(8,128)S(1)}, bf16[5,8,2,64,128]{4,3,2,1,0:T(8,128)(2,1)S(1)}, bf16[4,256,256]{2,1,0:T(8,128)(2,1)S(1)}, f32[1,256]{1,0:T(1,128)S(1)}) custom-call(bf16[4,14,28,2,2,64]{5,4,3,2,1,0:T(2,128)(2,1)} %bitcast.8, bf16[3,3,2,64]{3,2,1,0:T(2,128)(2,1)} %w1_hbm.1, f32[1,64]{1,0:T(1,128)} %bitcast.9, ...), custom_call_target="tpu_custom_call" | custom-call | tf_op jit(solution)/shard_map/conv/pallas_call | solution.py:527
  25.4 1.7 %tail.1 = f32[7,7,2,64,64]{4,3,2,1,0:T(8,128)} custom-call(f32[8,7,2,64,64]{4,3,2,1,0:T(8,128)S(1)} %get-tuple-element.9.tile, bf16[5,8,2,64,128]{4,3,2,1,0:T(8,128)(2,1)S(1)} %get-tuple-element.10.ymat, bf16[4,256,256]{2,1,0:T(8,128)(2,1)S(1)} %get-tuple-element.11.wt2, f32[1,256]{1,0:T(1,128)S(1)} %get-tuple-element.12.bias2), custom_call_target="tpu_custom_call" | custom-call | tf_op jit(solution)/shard_map/tail/pallas_call | solution.py:556

commit v26 on v25

--- a/solution.py
+++ b/solution.py
@@ -142,7 +142,7 @@
     to_rs = [lax.rem(r + k, n_rows) for k in range(n_rows)]
     for kr, kc in sorted(
         ((kr, kc) for kr in range(n_rows) for kc in range(n_cols) if kr or kc),
-        key=lambda k: (not (k[0] in (2, 3) and k[1] == 1), -(min(k[0], n_rows - k[0]) // 2 + min(k[1], n_cols - k[1]))),
+        key=lambda k: (k[1] not in (1, 2), k[0] not in (2, 3, 4, 5), k[1] == 2, k[0] < 4, -min(k[0], n_rows - k[0])),
     ):
         pl.semaphore_signal(barrier, inc=1, device_id=device(to_rs[kr], to_cs[kc]), device_id_type=MESH)
 

time: 27.2 us -> 27.1 us (level)
  no operation moved by 1% of the time
where the time goes in v26:
time: 27.1 us; the launch traced here: 27 us
  Pallas kernels  27 us (100%)
    pallas_call x1, Pallas kernels, run_local(): pl.pallas_call(functools.partial(conv_kernel, n_rows, n_cols), out_shape=...  25.3 us
    pallas_call x1, Pallas kernels, run_local(): pl.pallas_call(tail_kernel, out_shape=jax.ShapeDtypeStruct((tile_h, tile_...  1.71 us

profile of v26, /device:TPU:101, one launch (start us, length us, event | category | flops | bytes accessed | tf_op | source)
XLA Modules:
  0.0 27.0 jit_solution(9772703063325168946)
XLA Ops:
  0.0 25.3 %conv.1 = (f32[8,7,2,64,64]{4,3,2,1,0:T(8,128)S(1)}, bf16[5,8,2,64,128]{4,3,2,1,0:T(8,128)(2,1)S(1)}, bf16[4,256,256]{2,1,0:T(8,128)(2,1)S(1)}, f32[1,256]{1,0:T(1,128)S(1)}) custom-call(bf16[4,14,28,2,2,64]{5,4,3,2,1,0:T(2,128)(2,1)} %bitcast.8, bf16[3,3,2,64]{3,2,1,0:T(2,128)(2,1)} %w1_hbm.1, f32[1,64]{1,0:T(1,128)} %bitcast.9, ...), custom_call_target="tpu_custom_call" | custom-call | tf_op jit(solution)/shard_map/conv/pallas_call | solution.py:527
  25.3 1.7 %tail.1 = f32[7,7,2,64,64]{4,3,2,1,0:T(8,128)} custom-call(f32[8,7,2,64,64]{4,3,2,1,0:T(8,128)S(1)} %get-tuple-element.9.tile, bf16[5,8,2,64,128]{4,3,2,1,0:T(8,128)(2,1)S(1)} %get-tuple-element.10.ymat, bf16[4,256,256]{2,1,0:T(8,128)(2,1)S(1)} %get-tuple-element.11.wt2, f32[1,256]{1,0:T(1,128)S(1)} %get-tuple-element.12.bias2), custom_call_target="tpu_custom_call" | custom-call | tf_op jit(solution)/shard_map/tail/pallas_call | solution.py:556

commit v27 on v24

--- a/solution.py
+++ b/solution.py
@@ -14,7 +14,7 @@
 TURNS, FIRSTS, SECONDS = (2, 4, 5, 6), (1, 3, 4, 5), (0, 2, 3, 3)
 EARLY_FROM = 1
 AHEAD = (1, 0)
-CHIPS_ALONG = (3, 1, 2, 0)
+CHIPS_ALONG = (1, 3, 2, 0)
 CHIP_ORDER = tuple((other, dy) for other in (0, 1) for dy in (0, 1, -1, 2))
 
 

time: 25.5 us -> 25.8 us (1.012)
  the two profiles are of different devices: /device:TPU:97 before, /device:TPU:102 now
where the time goes in v27:
time: 25.8 us; the launch traced here: 25.7 us
  Pallas kernels  25.7 us (100%)
    pallas_call x1, Pallas kernels, run_local(): pl.pallas_call(functools.partial(conv_kernel, n_rows, n_cols), out_shape=...  24 us
    pallas_call x1, Pallas kernels, run_local(): pl.pallas_call(tail_kernel, out_shape=jax.ShapeDtypeStruct((tile_h, tile_...  1.71 us

profile of v27, /device:TPU:102, one launch (start us, length us, event | category | flops | bytes accessed | tf_op | source)
XLA Modules:
  0.0 25.7 jit_solution(12797294659864053936)
XLA Ops:
  0.0 24.0 %conv.1 = (f32[8,7,2,64,64]{4,3,2,1,0:T(8,128)S(1)}, bf16[5,8,2,64,128]{4,3,2,1,0:T(8,128)(2,1)S(1)}, bf16[4,256,256]{2,1,0:T(8,128)(2,1)S(1)}, f32[1,256]{1,0:T(1,128)S(1)}) custom-call(bf16[4,14,28,2,2,64]{5,4,3,2,1,0:T(2,128)(2,1)} %bitcast.8, bf16[3,3,2,64]{3,2,1,0:T(2,128)(2,1)} %w1_hbm.1, f32[1,64]{1,0:T(1,128)} %bitcast.9, ...), custom_call_target="tpu_custom_call" | custom-call | tf_op jit(solution)/shard_map/conv/pallas_call | solution.py:527
  24.0 1.7 %tail.1 = f32[7,7,2,64,64]{4,3,2,1,0:T(8,128)} custom-call(f32[8,7,2,64,64]{4,3,2,1,0:T(8,128)S(1)} %get-tuple-element.9.tile, bf16[5,8,2,64,128]{4,3,2,1,0:T(8,128)(2,1)S(1)} %get-tuple-element.10.ymat, bf16[4,256,256]{2,1,0:T(8,128)(2,1)S(1)} %get-tuple-element.11.wt2, f32[1,256]{1,0:T(1,128)S(1)} %get-tuple-element.12.bias2), custom_call_target="tpu_custom_call" | custom-call | tf_op jit(solution)/shard_map/tail/pallas_call | solution.py:556

commit v28 on v24

--- a/solution.py
+++ b/solution.py
@@ -295,7 +295,7 @@
 
         send_chip(0, t)
         send_tile(1, jnp.int32(ahead_r), jnp.int32(ahead_c), there & jnp.logical_not(is_ahead))
-        pl.when(t == 0)(send_weights)
+        pl.when(t == 1)(send_weights)
         return carry
 
     lax.fori_loop(0, chips, pack_and_send, 0)

time: 25.5 us -> 25.3 us (level)
  no operation moved by 1% of the time
where the time goes in v28:
time: 25.3 us; the launch traced here: 25.2 us
  Pallas kernels  25.2 us (100%)
    pallas_call x1, Pallas kernels, run_local(): pl.pallas_call(functools.partial(conv_kernel, n_rows, n_cols), out_shape=...  23.5 us
    pallas_call x1, Pallas kernels, run_local(): pl.pallas_call(tail_kernel, out_shape=jax.ShapeDtypeStruct((tile_h, tile_...  1.71 us

profile of v28, /device:TPU:97, one launch (start us, length us, event | category | flops | bytes accessed | tf_op | source)
XLA Modules:
  0.0 25.2 jit_solution(848943569642303873)
XLA Ops:
  0.0 23.5 %conv.1 = (f32[8,7,2,64,64]{4,3,2,1,0:T(8,128)S(1)}, bf16[5,8,2,64,128]{4,3,2,1,0:T(8,128)(2,1)S(1)}, bf16[4,256,256]{2,1,0:T(8,128)(2,1)S(1)}, f32[1,256]{1,0:T(1,128)S(1)}) custom-call(bf16[4,14,28,2,2,64]{5,4,3,2,1,0:T(2,128)(2,1)} %bitcast.8, bf16[3,3,2,64]{3,2,1,0:T(2,128)(2,1)} %w1_hbm.1, f32[1,64]{1,0:T(1,128)} %bitcast.9, ...), custom_call_target="tpu_custom_call" | custom-call | tf_op jit(solution)/shard_map/conv/pallas_call | solution.py:527
  23.5 1.7 %tail.1 = f32[7,7,2,64,64]{4,3,2,1,0:T(8,128)} custom-call(f32[8,7,2,64,64]{4,3,2,1,0:T(8,128)S(1)} %get-tuple-element.9.tile, bf16[5,8,2,64,128]{4,3,2,1,0:T(8,128)(2,1)S(1)} %get-tuple-element.10.ymat, bf16[4,256,256]{2,1,0:T(8,128)(2,1)S(1)} %get-tuple-element.11.wt2, f32[1,256]{1,0:T(1,128)S(1)} %get-tuple-element.12.bias2), custom_call_target="tpu_custom_call" | custom-call | tf_op jit(solution)/shard_map/tail/pallas_call | solution.py:556

commit v29 on v26

--- a/solution.py
+++ b/solution.py
@@ -15,7 +15,7 @@
 EARLY_FROM = 1
 AHEAD = (1, 0)
 CHIPS_ALONG = (3, 1, 2, 0)
-CHIP_ORDER = tuple((other, dy) for other in (0, 1) for dy in (1, -1, 0, 2))
+CHIP_ORDER = tuple((other, dy) for other in (0, 1) for dy in (0, 1, 2, -1))
 
 
 def turn(recv, i, put):

time: 27.1 us -> 25.4 us (0.937)
  the two profiles are of different devices: /device:TPU:101 before, /device:TPU:97 now
where the time goes in v29:
time: 25.4 us; the launch traced here: 25.3 us
  Pallas kernels  25.3 us (100%)
    pallas_call x1, Pallas kernels, run_local(): pl.pallas_call(functools.partial(conv_kernel, n_rows, n_cols), out_shape=...  23.6 us
    pallas_call x1, Pallas kernels, run_local(): pl.pallas_call(tail_kernel, out_shape=jax.ShapeDtypeStruct((tile_h, tile_...  1.71 us

profile of v29, /device:TPU:97, one launch (start us, length us, event | category | flops | bytes accessed | tf_op | source)
XLA Modules:
  0.0 25.3 jit_solution(9088527074579618308)
XLA Ops:
  0.0 23.6 %conv.1 = (f32[8,7,2,64,64]{4,3,2,1,0:T(8,128)S(1)}, bf16[5,8,2,64,128]{4,3,2,1,0:T(8,128)(2,1)S(1)}, bf16[4,256,256]{2,1,0:T(8,128)(2,1)S(1)}, f32[1,256]{1,0:T(1,128)S(1)}) custom-call(bf16[4,14,28,2,2,64]{5,4,3,2,1,0:T(2,128)(2,1)} %bitcast.8, bf16[3,3,2,64]{3,2,1,0:T(2,128)(2,1)} %w1_hbm.1, f32[1,64]{1,0:T(1,128)} %bitcast.9, ...), custom_call_target="tpu_custom_call" | custom-call | tf_op jit(solution)/shard_map/conv/pallas_call | solution.py:527
  23.6 1.7 %tail.1 = f32[7,7,2,64,64]{4,3,2,1,0:T(8,128)} custom-call(f32[8,7,2,64,64]{4,3,2,1,0:T(8,128)S(1)} %get-tuple-element.9.tile, bf16[5,8,2,64,128]{4,3,2,1,0:T(8,128)(2,1)S(1)} %get-tuple-element.10.ymat, bf16[4,256,256]{2,1,0:T(8,128)(2,1)S(1)} %get-tuple-element.11.wt2, f32[1,256]{1,0:T(1,128)S(1)} %get-tuple-element.12.bias2), custom_call_target="tpu_custom_call" | custom-call | tf_op jit(solution)/shard_map/tail/pallas_call | solution.py:556

commit v30 on v28

--- a/solution.py
+++ b/solution.py
@@ -489,17 +489,21 @@
     late = (rows - 2) * par
     here = 2 * (1 - par)
 
+    cut = out_hbm.shape[1] // 2
+
     def start(k, carry):
-        pltpu.make_async_copy(tile.at[par + k], out_hbm.at[k], sem.at[0]).start()
+        for part in (pl.ds(0, cut), pl.ds(cut, out_hbm.shape[1] - cut)):
+            pltpu.make_async_copy(tile.at[par + k, part], out_hbm.at[k, part], sem.at[0]).start()
         return carry
 
     lax.fori_loop(here, here + rows - 2, start, 0)
     i = (o_pairs - 1) * par
     second((ymat.at[i], ymat.at[i + 1]), lambda dw: wt2[dw], bias2[...], o_new)
-    last = pltpu.make_async_copy(o_new, out_hbm.at[pl.ds(late, 2)], sem.at[1])
-    last.start()
+    for k in range(2):
+        for part in (pl.ds(0, cut), pl.ds(cut, out_hbm.shape[1] - cut)):
+            pltpu.make_async_copy(o_new.at[k, part], out_hbm.at[late + k, part], sem.at[1]).start()
     pltpu.make_async_copy(tile.at[0 : rows - 2], out_hbm.at[0 : rows - 2], sem.at[0]).wait()
-    last.wait()
+    pltpu.make_async_copy(o_new, out_hbm.at[pl.ds(late, 2)], sem.at[1]).wait()
 
 
 def solution(mesh):

time: 25.3 us -> 25.3 us (level)
  no operation moved by 1% of the time
where the time goes in v30:
time: 25.3 us; the launch traced here: 25.2 us
  Pallas kernels  25.2 us (100%)
    pallas_call x1, Pallas kernels, run_local(): pl.pallas_call(functools.partial(conv_kernel, n_rows, n_cols), out_shape=...  23.5 us
    pallas_call x1, Pallas kernels, run_local(): pl.pallas_call(tail_kernel, out_shape=jax.ShapeDtypeStruct((tile_h, tile_...  1.7 us

profile of v30, /device:TPU:97, one launch (start us, length us, event | category | flops | bytes accessed | tf_op | source)
XLA Modules:
  0.0 25.2 jit_solution(16778150988918037123)
XLA Ops:
  0.0 23.5 %conv.1 = (f32[8,7,2,64,64]{4,3,2,1,0:T(8,128)S(1)}, bf16[5,8,2,64,128]{4,3,2,1,0:T(8,128)(2,1)S(1)}, bf16[4,256,256]{2,1,0:T(8,128)(2,1)S(1)}, f32[1,256]{1,0:T(1,128)S(1)}) custom-call(bf16[4,14,28,2,2,64]{5,4,3,2,1,0:T(2,128)(2,1)} %bitcast.8, bf16[3,3,2,64]{3,2,1,0:T(2,128)(2,1)} %w1_hbm.1, f32[1,64]{1,0:T(1,128)} %bitcast.9, ...), custom_call_target="tpu_custom_call" | custom-call | tf_op jit(solution)/shard_map/conv/pallas_call | solution.py:531
  23.5 1.7 %tail.1 = f32[7,7,2,64,64]{4,3,2,1,0:T(8,128)} custom-call(f32[8,7,2,64,64]{4,3,2,1,0:T(8,128)S(1)} %get-tuple-element.9.tile, bf16[5,8,2,64,128]{4,3,2,1,0:T(8,128)(2,1)S(1)} %get-tuple-element.10.ymat, bf16[4,256,256]{2,1,0:T(8,128)(2,1)S(1)} %get-tuple-element.11.wt2, f32[1,256]{1,0:T(1,128)S(1)} %get-tuple-element.12.bias2), custom_call_target="tpu_custom_call" | custom-call | tf_op jit(solution)/shard_map/tail/pallas_call | solution.py:560

commit v31 on v28

--- a/solution.py
+++ b/solution.py
@@ -14,7 +14,7 @@
 TURNS, FIRSTS, SECONDS = (2, 4, 5, 6), (1, 3, 4, 5), (0, 2, 3, 3)
 EARLY_FROM = 1
 AHEAD = (1, 0)
-CHIPS_ALONG = (3, 1, 2, 0)
+CHIPS_ALONG = (1, 3, 2, 0)
 CHIP_ORDER = tuple((other, dy) for other in (0, 1) for dy in (0, 1, -1, 2))
 
 

time: 25.3 us -> 26.5 us (1.047)
  the two profiles are of different devices: /device:TPU:97 before, /device:TPU:103 now
where the time goes in v31:
time: 26.5 us; the launch traced here: 26.4 us
  Pallas kernels  26.4 us (100%)
    pallas_call x1, Pallas kernels, run_local(): pl.pallas_call(functools.partial(conv_kernel, n_rows, n_cols), out_shape=...  24.7 us
    pallas_call x1, Pallas kernels, run_local(): pl.pallas_call(tail_kernel, out_shape=jax.ShapeDtypeStruct((tile_h, tile_...  1.71 us

profile of v31, /device:TPU:103, one launch (start us, length us, event | category | flops | bytes accessed | tf_op | source)
XLA Modules:
  0.0 26.4 jit_solution(6366787561080253557)
XLA Ops:
  0.0 24.7 %conv.1 = (f32[8,7,2,64,64]{4,3,2,1,0:T(8,128)S(1)}, bf16[5,8,2,64,128]{4,3,2,1,0:T(8,128)(2,1)S(1)}, bf16[4,256,256]{2,1,0:T(8,128)(2,1)S(1)}, f32[1,256]{1,0:T(1,128)S(1)}) custom-call(bf16[4,14,28,2,2,64]{5,4,3,2,1,0:T(2,128)(2,1)} %bitcast.8, bf16[3,3,2,64]{3,2,1,0:T(2,128)(2,1)} %w1_hbm.1, f32[1,64]{1,0:T(1,128)} %bitcast.9, ...), custom_call_target="tpu_custom_call" | custom-call | tf_op jit(solution)/shard_map/conv/pallas_call | solution.py:527
  24.7 1.7 %tail.1 = f32[7,7,2,64,64]{4,3,2,1,0:T(8,128)} custom-call(f32[8,7,2,64,64]{4,3,2,1,0:T(8,128)S(1)} %get-tuple-element.9.tile, bf16[5,8,2,64,128]{4,3,2,1,0:T(8,128)(2,1)S(1)} %get-tuple-element.10.ymat, bf16[4,256,256]{2,1,0:T(8,128)(2,1)S(1)} %get-tuple-element.11.wt2, f32[1,256]{1,0:T(1,128)S(1)} %get-tuple-element.12.bias2), custom_call_target="tpu_custom_call" | custom-call | tf_op jit(solution)/shard_map/tail/pallas_call | solution.py:556

commit v32 on v28

--- a/solution.py
+++ b/solution.py
@@ -295,7 +295,7 @@
 
         send_chip(0, t)
         send_tile(1, jnp.int32(ahead_r), jnp.int32(ahead_c), there & jnp.logical_not(is_ahead))
-        pl.when(t == 1)(send_weights)
+        pl.when(t == 2)(send_weights)
         return carry
 
     lax.fori_loop(0, chips, pack_and_send, 0)

time: 25.3 us -> 26.3 us (1.040)
  Pallas kernels: 25.2 us -> 26.2 us
    pallas_call x1, Pallas kernels: 23.5 us -> 24.5 us  [run_local(): pl.pallas_call(functools.partial(conv_kernel, n_rows, n_cols), out_shape=...]
where the time goes in v32:
time: 26.3 us; the launch traced here: 26.2 us
  Pallas kernels  26.2 us (100%)
    pallas_call x1, Pallas kernels, run_local(): pl.pallas_call(functools.partial(conv_kernel, n_rows, n_cols), out_shape=...  24.5 us
    pallas_call x1, Pallas kernels, run_local(): pl.pallas_call(tail_kernel, out_shape=jax.ShapeDtypeStruct((tile_h, tile_...  1.71 us

profile of v32, /device:TPU:97, one launch (start us, length us, event | category | flops | bytes accessed | tf_op | source)
XLA Modules:
  0.0 26.2 jit_solution(1308070087980233856)
XLA Ops:
  0.0 24.5 %conv.1 = (f32[8,7,2,64,64]{4,3,2,1,0:T(8,128)S(1)}, bf16[5,8,2,64,128]{4,3,2,1,0:T(8,128)(2,1)S(1)}, bf16[4,256,256]{2,1,0:T(8,128)(2,1)S(1)}, f32[1,256]{1,0:T(1,128)S(1)}) custom-call(bf16[4,14,28,2,2,64]{5,4,3,2,1,0:T(2,128)(2,1)} %bitcast.8, bf16[3,3,2,64]{3,2,1,0:T(2,128)(2,1)} %w1_hbm.1, f32[1,64]{1,0:T(1,128)} %bitcast.9, ...), custom_call_target="tpu_custom_call" | custom-call | tf_op jit(solution)/shard_map/conv/pallas_call | solution.py:527
  24.5 1.7 %tail.1 = f32[7,7,2,64,64]{4,3,2,1,0:T(8,128)} custom-call(f32[8,7,2,64,64]{4,3,2,1,0:T(8,128)S(1)} %get-tuple-element.9.tile, bf16[5,8,2,64,128]{4,3,2,1,0:T(8,128)(2,1)S(1)} %get-tuple-element.10.ymat, bf16[4,256,256]{2,1,0:T(8,128)(2,1)S(1)} %get-tuple-element.11.wt2, f32[1,256]{1,0:T(1,128)S(1)} %get-tuple-element.12.bias2), custom_call_target="tpu_custom_call" | custom-call | tf_op jit(solution)/shard_map/tail/pallas_call | solution.py:556

commit v33 on v30

--- a/solution.py
+++ b/solution.py
@@ -15,7 +15,7 @@
 EARLY_FROM = 1
 AHEAD = (1, 0)
 CHIPS_ALONG = (3, 1, 2, 0)
-CHIP_ORDER = tuple((other, dy) for other in (0, 1) for dy in (0, 1, -1, 2))
+CHIP_ORDER = tuple((other, dy) for other in (0, 1) for dy in (0, 1, 2, -1))
 
 
 def turn(recv, i, put):

time: 25.3 us -> 25.6 us (1.012)
  Pallas kernels: 25.2 us -> 25.5 us
    pallas_call x1, Pallas kernels: 23.5 us -> 23.8 us  [run_local(): pl.pallas_call(functools.partial(conv_kernel, n_rows, n_cols), out_shape=...]
where the time goes in v33:
time: 25.6 us; the launch traced here: 25.5 us
  Pallas kernels  25.5 us (100%)
    pallas_call x1, Pallas kernels, run_local(): pl.pallas_call(functools.partial(conv_kernel, n_rows, n_cols), out_shape=...  23.8 us
    pallas_call x1, Pallas kernels, run_local(): pl.pallas_call(tail_kernel, out_shape=jax.ShapeDtypeStruct((tile_h, tile_...  1.7 us

profile of v33, /device:TPU:97, one launch (start us, length us, event | category | flops | bytes accessed | tf_op | source)
XLA Modules:
  0.0 25.5 jit_solution(4845258617458361143)
XLA Ops:
  0.0 23.8 %conv.1 = (f32[8,7,2,64,64]{4,3,2,1,0:T(8,128)S(1)}, bf16[5,8,2,64,128]{4,3,2,1,0:T(8,128)(2,1)S(1)}, bf16[4,256,256]{2,1,0:T(8,128)(2,1)S(1)}, f32[1,256]{1,0:T(1,128)S(1)}) custom-call(bf16[4,14,28,2,2,64]{5,4,3,2,1,0:T(2,128)(2,1)} %bitcast.8, bf16[3,3,2,64]{3,2,1,0:T(2,128)(2,1)} %w1_hbm.1, f32[1,64]{1,0:T(1,128)} %bitcast.9, ...), custom_call_target="tpu_custom_call" | custom-call | tf_op jit(solution)/shard_map/conv/pallas_call | solution.py:531
  23.8 1.7 %tail.1 = f32[7,7,2,64,64]{4,3,2,1,0:T(8,128)} custom-call(f32[8,7,2,64,64]{4,3,2,1,0:T(8,128)S(1)} %get-tuple-element.9.tile, bf16[5,8,2,64,128]{4,3,2,1,0:T(8,128)(2,1)S(1)} %get-tuple-element.10.ymat, bf16[4,256,256]{2,1,0:T(8,128)(2,1)S(1)} %get-tuple-element.11.wt2, f32[1,256]{1,0:T(1,128)S(1)} %get-tuple-element.12.bias2), custom_call_target="tpu_custom_call" | custom-call | tf_op jit(solution)/shard_map/tail/pallas_call | solution.py:560

commit v34 on v30

--- a/solution.py
+++ b/solution.py
@@ -272,17 +272,24 @@
     pl.semaphore_wait(barrier, sources - 1)
 
     def send_weights():
-        for kr in range(0, n_rows, 2):
+        def body(k, carry):
+            to_r = lax.rem(r + 2 * k, n_rows)
             for kc in range(n_cols):
-                if kr or kc:
+
+                def copy(kc=kc):
                     pltpu.make_async_remote_copy(
                         src_ref=w1own,
                         dst_ref=w1all.at[r // 2, par, c],
                         send_sem=wsend_sem,
                         recv_sem=wrecv_sem,
-                        device_id=device(to_rs[kr], to_cs[kc]),
+                        device_id=device(to_r, to_cs[kc]),
                         device_id_type=MESH,
                     ).start()
+
+                pl.when(k < chips)(copy) if kc == 0 else copy()
+            return carry
+
+        lax.fori_loop(1, chips + 1, body, 0)
 
     def pack_and_send(t, carry):
         pl.when(t < chips - 1)(lambda: pack_rows(turn_to(t + 1)[0], *groups[0][0]))

time: 25.3 us -> 26 us (1.028)
  the two profiles are of different devices: /device:TPU:97 before, /device:TPU:107 now
where the time goes in v34:
time: 26 us
  Pallas kernels  25.9 us (100%)
    pallas_call x1, Pallas kernels, run_local(): pl.pallas_call(functools.partial(conv_kernel, n_rows, n_cols), out_shape=...  24.2 us
    pallas_call x1, Pallas kernels, run_local(): pl.pallas_call(tail_kernel, out_shape=jax.ShapeDtypeStruct((tile_h, tile_...  1.7 us

profile of v34, /device:TPU:107, one launch (start us, length us, event | category | flops | bytes accessed | tf_op | source)
XLA Modules:
  0.0 26.0 jit_solution(12812225896167937546)
XLA Ops:
  0.0 24.2 %conv.1 = (f32[8,7,2,64,64]{4,3,2,1,0:T(8,128)S(1)}, bf16[5,8,2,64,128]{4,3,2,1,0:T(8,128)(2,1)S(1)}, bf16[4,256,256]{2,1,0:T(8,128)(2,1)S(1)}, f32[1,256]{1,0:T(1,128)S(1)}) custom-call(bf16[4,14,28,2,2,64]{5,4,3,2,1,0:T(2,128)(2,1)} %bitcast.8, bf16[3,3,2,64]{3,2,1,0:T(2,128)(2,1)} %w1_hbm.1, f32[1,64]{1,0:T(1,128)} %bitcast.9, ...), custom_call_target="tpu_custom_call" | custom-call | tf_op jit(solution)/shard_map/conv/pallas_call | solution.py:538
  24.3 1.7 %tail.1 = f32[7,7,2,64,64]{4,3,2,1,0:T(8,128)} custom-call(f32[8,7,2,64,64]{4,3,2,1,0:T(8,128)S(1)} %get-tuple-element.9.tile, bf16[5,8,2,64,128]{4,3,2,1,0:T(8,128)(2,1)S(1)} %get-tuple-element.10.ymat, bf16[4,256,256]{2,1,0:T(8,128)(2,1)S(1)} %get-tuple-element.11.wt2, f32[1,256]{1,0:T(1,128)S(1)} %get-tuple-element.12.bias2), custom_call_target="tpu_custom_call" | custom-call | tf_op jit(solution)/shard_map/tail/pallas_call | solution.py:567

commit v35 on v30

--- a/solution.py
+++ b/solution.py
@@ -14,7 +14,7 @@
 TURNS, FIRSTS, SECONDS = (2, 4, 5, 6), (1, 3, 4, 5), (0, 2, 3, 3)
 EARLY_FROM = 1
 AHEAD = (1, 0)
-CHIPS_ALONG = (3, 1, 2, 0)
+CHIPS_ALONG = (3, 1, 0, 2)
 CHIP_ORDER = tuple((other, dy) for other in (0, 1) for dy in (0, 1, -1, 2))
 
 

time: 25.3 us -> 26.2 us (1.036)
  the two profiles are of different devices: /device:TPU:97 before, /device:TPU:101 now
where the time goes in v35:
time: 26.2 us; the launch traced here: 26.1 us
  Pallas kernels  26.1 us (100%)
    pallas_call x1, Pallas kernels, run_local(): pl.pallas_call(functools.partial(conv_kernel, n_rows, n_cols), out_shape=...  24.4 us
    pallas_call x1, Pallas kernels, run_local(): pl.pallas_call(tail_kernel, out_shape=jax.ShapeDtypeStruct((tile_h, tile_...  1.7 us

profile of v35, /device:TPU:101, one launch (start us, length us, event | category | flops | bytes accessed | tf_op | source)
XLA Modules:
  0.0 26.1 jit_solution(10151646695868663823)
XLA Ops:
  0.0 24.4 %conv.1 = (f32[8,7,2,64,64]{4,3,2,1,0:T(8,128)S(1)}, bf16[5,8,2,64,128]{4,3,2,1,0:T(8,128)(2,1)S(1)}, bf16[4,256,256]{2,1,0:T(8,128)(2,1)S(1)}, f32[1,256]{1,0:T(1,128)S(1)}) custom-call(bf16[4,14,28,2,2,64]{5,4,3,2,1,0:T(2,128)(2,1)} %bitcast.8, bf16[3,3,2,64]{3,2,1,0:T(2,128)(2,1)} %w1_hbm.1, f32[1,64]{1,0:T(1,128)} %bitcast.9, ...), custom_call_target="tpu_custom_call" | custom-call | tf_op jit(solution)/shard_map/conv/pallas_call | solution.py:531
  24.4 1.7 %tail.1 = f32[7,7,2,64,64]{4,3,2,1,0:T(8,128)} custom-call(f32[8,7,2,64,64]{4,3,2,1,0:T(8,128)S(1)} %get-tuple-element.9.tile, bf16[5,8,2,64,128]{4,3,2,1,0:T(8,128)(2,1)S(1)} %get-tuple-element.10.ymat, bf16[4,256,256]{2,1,0:T(8,128)(2,1)S(1)} %get-tuple-element.11.wt2, f32[1,256]{1,0:T(1,128)S(1)} %get-tuple-element.12.bias2), custom_call_target="tpu_custom_call" | custom-call | tf_op jit(solution)/shard_map/tail/pallas_call | solution.py:560

commit v36 on v33

--- a/solution.py
+++ b/solution.py
@@ -15,7 +15,7 @@
 EARLY_FROM = 1
 AHEAD = (1, 0)
 CHIPS_ALONG = (3, 1, 2, 0)
-CHIP_ORDER = tuple((other, dy) for other in (0, 1) for dy in (0, 1, 2, -1))
+CHIP_ORDER = tuple((other, dy) for other in (0, 1) for dy in (0, -1, 1, 2))
 
 
 def turn(recv, i, put):

time: 25.6 us -> 25.7 us (level); the launches traced: 25.5 us -> 25.2 us
  Pallas kernels: 25.5 us -> 25.2 us
    pallas_call x1, Pallas kernels: 23.8 us -> 23.5 us  [run_local(): pl.pallas_call(functools.partial(conv_kernel, n_rows, n_cols), out_shape=...]
where the time goes in v36:
time: 25.7 us; the launch traced here: 25.2 us
  Pallas kernels  25.2 us (98%)
    pallas_call x1, Pallas kernels, run_local(): pl.pallas_call(functools.partial(conv_kernel, n_rows, n_cols), out_shape=...  23.5 us
    pallas_call x1, Pallas kernels, run_local(): pl.pallas_call(tail_kernel, out_shape=jax.ShapeDtypeStruct((tile_h, tile_...  1.7 us

profile of v36, /device:TPU:97, one launch (start us, length us, event | category | flops | bytes accessed | tf_op | source)
XLA Modules:
  0.0 25.2 jit_solution(11583252316640451673)
XLA Ops:
  0.0 23.5 %conv.1 = (f32[8,7,2,64,64]{4,3,2,1,0:T(8,128)S(1)}, bf16[5,8,2,64,128]{4,3,2,1,0:T(8,128)(2,1)S(1)}, bf16[4,256,256]{2,1,0:T(8,128)(2,1)S(1)}, f32[1,256]{1,0:T(1,128)S(1)}) custom-call(bf16[4,14,28,2,2,64]{5,4,3,2,1,0:T(2,128)(2,1)} %bitcast.8, bf16[3,3,2,64]{3,2,1,0:T(2,128)(2,1)} %w1_hbm.1, f32[1,64]{1,0:T(1,128)} %bitcast.9, ...), custom_call_target="tpu_custom_call" | custom-call | tf_op jit(solution)/shard_map/conv/pallas_call | solution.py:531
  23.5 1.7 %tail.1 = f32[7,7,2,64,64]{4,3,2,1,0:T(8,128)} custom-call(f32[8,7,2,64,64]{4,3,2,1,0:T(8,128)S(1)} %get-tuple-element.9.tile, bf16[5,8,2,64,128]{4,3,2,1,0:T(8,128)(2,1)S(1)} %get-tuple-element.10.ymat, bf16[4,256,256]{2,1,0:T(8,128)(2,1)S(1)} %get-tuple-element.11.wt2, f32[1,256]{1,0:T(1,128)S(1)} %get-tuple-element.12.bias2), custom_call_target="tpu_custom_call" | custom-call | tf_op jit(solution)/shard_map/tail/pallas_call | solution.py:560

commit v37 on v30

--- a/solution.py
+++ b/solution.py
@@ -489,10 +489,11 @@
     late = (rows - 2) * par
     here = 2 * (1 - par)
 
-    cut = out_hbm.shape[1] // 2
+    width = out_hbm.shape[1]
+    parts = [pl.ds(j, min(2, width - j)) for j in range(0, width, 2)]
 
     def start(k, carry):
-        for part in (pl.ds(0, cut), pl.ds(cut, out_hbm.shape[1] - cut)):
+        for part in parts:
             pltpu.make_async_copy(tile.at[par + k, part], out_hbm.at[k, part], sem.at[0]).start()
         return carry
 
@@ -500,7 +501,7 @@
     i = (o_pairs - 1) * par
     second((ymat.at[i], ymat.at[i + 1]), lambda dw: wt2[dw], bias2[...], o_new)
     for k in range(2):
-        for part in (pl.ds(0, cut), pl.ds(cut, out_hbm.shape[1] - cut)):
+        for part in parts:
             pltpu.make_async_copy(o_new.at[k, part], out_hbm.at[late + k, part], sem.at[1]).start()
     pltpu.make_async_copy(tile.at[0 : rows - 2], out_hbm.at[0 : rows - 2], sem.at[0]).wait()
     pltpu.make_async_copy(o_new, out_hbm.at[pl.ds(late, 2)], sem.at[1]).wait()

time: 25.3 us -> 25.3 us (level)
  no operation moved by 1% of the time
where the time goes in v37:
time: 25.3 us; the launch traced here: 25.2 us
  Pallas kernels  25.2 us (100%)
    pallas_call x1, Pallas kernels, run_local(): pl.pallas_call(functools.partial(conv_kernel, n_rows, n_cols), out_shape=...  23.5 us
    pallas_call x1, Pallas kernels, run_local(): pl.pallas_call(tail_kernel, out_shape=jax.ShapeDtypeStruct((tile_h, tile_...  1.68 us

profile of v37, /device:TPU:97, one launch (start us, length us, event | category | flops | bytes accessed | tf_op | source)
XLA Modules:
  0.0 25.2 jit_solution(3373061897210175605)
XLA Ops:
  0.0 23.5 %conv.1 = (f32[8,7,2,64,64]{4,3,2,1,0:T(8,128)S(1)}, bf16[5,8,2,64,128]{4,3,2,1,0:T(8,128)(2,1)S(1)}, bf16[4,256,256]{2,1,0:T(8,128)(2,1)S(1)}, f32[1,256]{1,0:T(1,128)S(1)}) custom-call(bf16[4,14,28,2,2,64]{5,4,3,2,1,0:T(2,128)(2,1)} %bitcast.8, bf16[3,3,2,64]{3,2,1,0:T(2,128)(2,1)} %w1_hbm.1, f32[1,64]{1,0:T(1,128)} %bitcast.9, ...), custom_call_target="tpu_custom_call" | custom-call | tf_op jit(solution)/shard_map/conv/pallas_call | solution.py:532
  23.5 1.7 %tail.1 = f32[7,7,2,64,64]{4,3,2,1,0:T(8,128)} custom-call(f32[8,7,2,64,64]{4,3,2,1,0:T(8,128)S(1)} %get-tuple-element.9.tile, bf16[5,8,2,64,128]{4,3,2,1,0:T(8,128)(2,1)S(1)} %get-tuple-element.10.ymat, bf16[4,256,256]{2,1,0:T(8,128)(2,1)S(1)} %get-tuple-element.11.wt2, f32[1,256]{1,0:T(1,128)S(1)} %get-tuple-element.12.bias2), custom_call_target="tpu_custom_call" | custom-call | tf_op jit(solution)/shard_map/tail/pallas_call | solution.py:561

commit v38 on v37

--- a/solution.py
+++ b/solution.py
@@ -490,7 +490,7 @@
     here = 2 * (1 - par)
 
     width = out_hbm.shape[1]
-    parts = [pl.ds(j, min(2, width - j)) for j in range(0, width, 2)]
+    parts = [pl.ds(j, 1) for j in range(width)]
 
     def start(k, carry):
         for part in parts:

time: 25.3 us -> 25.3 us (level)
  no operation moved by 1% of the time
where the time goes in v38:
time: 25.3 us; the launch traced here: 25.2 us
  Pallas kernels  25.2 us (100%)
    pallas_call x1, Pallas kernels, run_local(): pl.pallas_call(functools.partial(conv_kernel, n_rows, n_cols), out_shape=...  23.5 us
    pallas_call x1, Pallas kernels, run_local(): pl.pallas_call(tail_kernel, out_shape=jax.ShapeDtypeStruct((tile_h, tile_...  1.67 us

profile of v38, /device:TPU:97, one launch (start us, length us, event | category | flops | bytes accessed | tf_op | source)
XLA Modules:
  0.0 25.2 jit_solution(12007190795300451129)
XLA Ops:
  0.0 23.5 %conv.1 = (f32[8,7,2,64,64]{4,3,2,1,0:T(8,128)S(1)}, bf16[5,8,2,64,128]{4,3,2,1,0:T(8,128)(2,1)S(1)}, bf16[4,256,256]{2,1,0:T(8,128)(2,1)S(1)}, f32[1,256]{1,0:T(1,128)S(1)}) custom-call(bf16[4,14,28,2,2,64]{5,4,3,2,1,0:T(2,128)(2,1)} %bitcast.8, bf16[3,3,2,64]{3,2,1,0:T(2,128)(2,1)} %w1_hbm.1, f32[1,64]{1,0:T(1,128)} %bitcast.9, ...), custom_call_target="tpu_custom_call" | custom-call | tf_op jit(solution)/shard_map/conv/pallas_call | solution.py:532
  23.5 1.7 %tail.1 = f32[7,7,2,64,64]{4,3,2,1,0:T(8,128)} custom-call(f32[8,7,2,64,64]{4,3,2,1,0:T(8,128)S(1)} %get-tuple-element.9.tile, bf16[5,8,2,64,128]{4,3,2,1,0:T(8,128)(2,1)S(1)} %get-tuple-element.10.ymat, bf16[4,256,256]{2,1,0:T(8,128)(2,1)S(1)} %get-tuple-element.11.wt2, f32[1,256]{1,0:T(1,128)S(1)} %get-tuple-element.12.bias2), custom_call_target="tpu_custom_call" | custom-call | tf_op jit(solution)/shard_map/tail/pallas_call | solution.py:561

commit v39 on v38

--- a/solution.py
+++ b/solution.py
@@ -490,11 +490,11 @@
     here = 2 * (1 - par)
 
     width = out_hbm.shape[1]
-    parts = [pl.ds(j, 1) for j in range(width)]
+    parts = [(pl.ds(j, 1), pl.ds(b, 1)) for j in range(width) for b in range(2)]
 
     def start(k, carry):
         for part in parts:
-            pltpu.make_async_copy(tile.at[par + k, part], out_hbm.at[k, part], sem.at[0]).start()
+            pltpu.make_async_copy(tile.at[(par + k, *part)], out_hbm.at[(k, *part)], sem.at[0]).start()
         return carry
 
     lax.fori_loop(here, here + rows - 2, start, 0)
@@ -502,7 +502,7 @@
     second((ymat.at[i], ymat.at[i + 1]), lambda dw: wt2[dw], bias2[...], o_new)
     for k in range(2):
         for part in parts:
-            pltpu.make_async_copy(o_new.at[k, part], out_hbm.at[late + k, part], sem.at[1]).start()
+            pltpu.make_async_copy(o_new.at[(k, *part)], out_hbm.at[(late + k, *part)], sem.at[1]).start()
     pltpu.make_async_copy(tile.at[0 : rows - 2], out_hbm.at[0 : rows - 2], sem.at[0]).wait()
     pltpu.make_async_copy(o_new, out_hbm.at[pl.ds(late, 2)], sem.at[1]).wait()
 

time: 25.3 us -> 25.3 us (level)
  no operation moved by 1% of the time
where the time goes in v39:
time: 25.3 us; the launch traced here: 25.2 us
  Pallas kernels  25.2 us (100%)
    pallas_call x1, Pallas kernels, run_local(): pl.pallas_call(functools.partial(conv_kernel, n_rows, n_cols), out_shape=...  23.5 us
    pallas_call x1, Pallas kernels, run_local(): pl.pallas_call(tail_kernel, out_shape=jax.ShapeDtypeStruct((tile_h, tile_...  1.67 us

profile of v39, /device:TPU:97, one launch (start us, length us, event | category | flops | bytes accessed | tf_op | source)
XLA Modules:
  0.0 25.2 jit_solution(2549512397666527161)
XLA Ops:
  0.0 23.5 %conv.1 = (f32[8,7,2,64,64]{4,3,2,1,0:T(8,128)S(1)}, bf16[5,8,2,64,128]{4,3,2,1,0:T(8,128)(2,1)S(1)}, bf16[4,256,256]{2,1,0:T(8,128)(2,1)S(1)}, f32[1,256]{1,0:T(1,128)S(1)}) custom-call(bf16[4,14,28,2,2,64]{5,4,3,2,1,0:T(2,128)(2,1)} %bitcast.8, bf16[3,3,2,64]{3,2,1,0:T(2,128)(2,1)} %w1_hbm.1, f32[1,64]{1,0:T(1,128)} %bitcast.9, ...), custom_call_target="tpu_custom_call" | custom-call | tf_op jit(solution)/shard_map/conv/pallas_call | solution.py:532
  23.5 1.7 %tail.1 = f32[7,7,2,64,64]{4,3,2,1,0:T(8,128)} custom-call(f32[8,7,2,64,64]{4,3,2,1,0:T(8,128)S(1)} %get-tuple-element.9.tile, bf16[5,8,2,64,128]{4,3,2,1,0:T(8,128)(2,1)S(1)} %get-tuple-element.10.ymat, bf16[4,256,256]{2,1,0:T(8,128)(2,1)S(1)} %get-tuple-element.11.wt2, f32[1,256]{1,0:T(1,128)S(1)} %get-tuple-element.12.bias2), custom_call_target="tpu_custom_call" | custom-call | tf_op jit(solution)/shard_map/tail/pallas_call | solution.py:561
